TPU v7x, 32 devices: a whole 2x2x4 slice. The times are simulated.
32 devices in a mesh: vp: 32 (over z, y, x, core).
Axes of the slice: x: 2, y: 2, z: 4, core: 2. Of those that a mesh axis runs over, the one named last changes fastest.
Arguments:
- residual: bfloat16 [8192, 4096], replicated
- labels: int32 [8192], replicated
- loss_mask: float32 [8192], replicated
- norm_gain: float32 [4096], replicated
- embed_table: bfloat16 [49408, 4096], P('vp')
Outputs:
- output 1: float32 [], replicated
- output 2: float32 [8192, 4096], P('vp')
- output 3: float32 [49408, 4096], P('vp')
- output 4: float32 [4096], replicated
All inputs are finite; a program needn't handle non-finite values.
Results may differ from a plain program's by a relative error of at most 0.001.
Values sent between devices are 32-bit elements.
A program may use at most 1 GiB of HBM per device.

v0:
```python
import jax
import jax.numpy as jnp
from jax import lax
from jax.sharding import PartitionSpec as P

VOCAB_REAL = 49155
LOGIT_SCALE = 6.0
NORM_EPS = 1e-6


def solution(mesh):
    vp_axis = mesh.axis_names[0]
    group_size = mesh.shape[vp_axis]

    def local_step(residual, labels, loss_mask, norm_gain, table_shard):
        tokens = residual.shape[0]
        shard_rows = table_shard.shape[0]
        tok_rows = tokens // group_size
        my_index = lax.axis_index(vp_axis)
        x_f32 = residual.astype(jnp.float32)
        inv_rms = lax.rsqrt(jnp.mean(x_f32 * x_f32, axis=-1, keepdims=True) + NORM_EPS)
        x_hat = x_f32 * inv_rms
        hidden = (x_hat * norm_gain).astype(jnp.bfloat16)
        logits = jnp.einsum('td,vd->tv', hidden, table_shard, preferred_element_type=jnp.float32) / LOGIT_SCALE
        col_ids = my_index * shard_rows + lax.broadcasted_iota(jnp.int32, (1, shard_rows), 1)
        logits = jnp.where(col_ids < VOCAB_REAL, logits, -jnp.inf)
        row_max = lax.pmax(jnp.max(logits, axis=-1), vp_axis)
        shifted = jnp.exp(logits - row_max[:, None])
        is_label = col_ids == labels[:, None]
        part_stats = jnp.stack([jnp.sum(shifted, axis=-1), jnp.sum(jnp.where(is_label, logits, 0.0), axis=-1)])
        row_stats = lax.psum(part_stats, vp_axis)
        sum_exp = row_stats[0]
        log_norm = row_max + jnp.log(sum_exp)
        mask_total = jnp.sum(loss_mask)
        tok_weight = loss_mask / mask_total
        mean_loss = jnp.sum(loss_mask * (log_norm - row_stats[1])) / mask_total
        row_prob = shifted / sum_exp[:, None]
        d_logits = (jnp.where(is_label, row_prob - 1.0, row_prob) * tok_weight[:, None]).astype(jnp.bfloat16)
        d_part = jnp.dot(d_logits, table_shard, preferred_element_type=jnp.float32) / LOGIT_SCALE
        d_embed = jnp.einsum('tv,td->vd', d_logits, hidden, preferred_element_type=jnp.float32) / LOGIT_SCALE
        d_hidden = lax.psum_scatter(d_part, vp_axis, scatter_dimension=0, tiled=True)
        x_hat_loc = lax.dynamic_slice_in_dim(x_hat, my_index * tok_rows, tok_rows, axis=0)
        inv_loc = lax.dynamic_slice_in_dim(inv_rms, my_index * tok_rows, tok_rows, axis=0)
        d_gain = lax.psum(jnp.sum(d_hidden * x_hat_loc, axis=0), vp_axis)
        value_a6 = d_hidden * norm_gain
        d_residual = inv_loc * (value_a6 - x_hat_loc * jnp.mean(value_a6 * x_hat_loc, axis=-1, keepdims=True))
        return mean_loss, d_residual, d_embed, d_gain

    return jax.shard_map(local_step, mesh=mesh, in_specs=(P(), P(), P(), P(), P(vp_axis, None)), out_specs=(P(), P(vp_axis, None), P(vp_axis, None), P()), check_vma=False)
```

profile of v0, /device:TPU:0, one launch (start us, length us, event | category | flops | bytes accessed | tf_op | source)
XLA Modules:
  0.0 1954.0 jit_solution(6193582049685920346)
XLA Ops:
  7.2 0.0 copy-start.5
  7.2 0.0 all-reduce.3.cloned.1.call-start
  7.2 0.6 iota_add_fusion
  7.8 20.9 %fusion = f32[8192]{0:T(1024)S(1)} fusion(bf16[8192,4096]{1,0:T(8,128)(2,1)} %param.5), kind=kLoop, calls=%fused_computation.2 | loop fusion | flops 100655104 | bytes 67141632 | tf_op jit(solution)/shard_map/reduce_sum | solution.py:21
  28.8 0.0 copy-done.5
  28.8 0.0 copy-start
  28.8 0.0 copy-start.2
  28.8 0.0 copy-start.4
  28.8 121.2 %fusion.11 = (f32[8192]{0:T(1024)S(1)}, f32[8192,1544]{0,1:T(8,128)}) fusion(bf16[1544,4096]{1,0:T(8,128)(2,1)} %param.9, f32[4096]{0:T(1024)S(1)} %copy-done.5, f32[8192]{0:T(1024)S(1)} %add_rsqrt_fusion, bf16[8192,4096]{1,0:T(8,128)(2,1)} %param.5, pred[1544]{0:T(1024)(128)(4,1)S(1)} %broadcast_compare_fusion), kind=kOutput, calls=%fused_computation.27 | convolution fusion | flops 103788240896 | bytes 130434568 | tf_op jit(solution)/shard_map/td,vd->tv/dot_general | solution.py:24
  150.0 0.0 copy-done
  150.0 42.0 %pmax.7 = f32[8192]{0:T(1024)S(1)} all-reduce(f32[8192]{0:T(1024)S(1)} %get-tuple-element.12), channel_id=1, replica_groups=mesh['vp'=32] {'vp'}, use_global_device_ids=true, to_apply=%region_2.3 | all-reduce | flops 8192 | bytes 65536 | tf_op jit(solution)/shard_map/pmax | solution.py:27
  192.0 0.0 copy-done.2
  192.0 0.0 copy-done.4
  192.0 22.9 %fusion.4 = (f32[8192]{0:T(1024)S(1)}, f32[8192]{0:T(1024)S(1)}) fusion(f32[8192,1544]{0,1:T(8,128)} %get-tuple-element.13, f32[8192]{0:T(1024)S(1)} %pmax.7, s32[8192]{0:T(1024)S(1)} %copy-done.2, s32[1544]{0:T(1024)S(1)} %copy-done.4), kind=kLoop, calls=%fused_computation.12 | loop fusion | flops 63225856 | bytes 50731040 | tf_op jit(solution)/shard_map/reduce_sum | solution.py:30
  215.0 0.7 pad_maximum_fusion
  215.7 0.0 all-reduce.3.cloned.1.call-update
  215.7 0.2 reduce-scatter.5.cloned.1.call-start
  215.9 127.2 %all-reduce.3.cloned.1.call-done = f32[2,8192]{1,0:T(2,128)} async-done(((f32[2,8192]{1,0:T(2,128)}), f32[2,8192]{1,0:T(2,128)}) %all-reduce.3.cloned.1.call-update) | async-done | bytes 65552 | tf_op jit(solution)/shard_map/psum | solution.py:31
  343.1 1.0 fusion.10
  344.1 0.6 fusion.9
  344.7 0.7 broadcast_divide_fusion
  345.4 143.8 %convolution_multiply_fusion = f32[8192,4096]{1,0:T(8,128)} fusion(bf16[1544,4096]{1,0:T(8,128)(2,1)} %param.9, f32[8192,1544]{0,1:T(8,128)} %get-tuple-element.13, f32[8192]{0:T(1024)S(1)} %broadcast_divide_fusion, f32[8192]{0:T(1024)S(1)} %bitcast.10, s32[8192]{0:T(1024)S(1)} %copy-done.2, f32[8192]{0:T(1024)S(1)} %pmax.7, s32[1544]{0:T(1024)S(1)} %copy-done.4), kind=kOutput, calls=%fused_computation.4 | convolution fusion | flops 103738179584 | bytes 197597216 | tf_op jit(solution)/shard_map/dot_general | solution.py:39
  489.2 0.0 reduce-scatter.5.cloned.1.call-update
  489.2 0.7 copy-done.1
  490.0 0.6 dynamic-slice.3
  490.6 66.1 %convert_multiply_fusion = f32[8192,4096]{1,0:T(8,128)} fusion(bf16[8192,4096]{1,0:T(8,128)(2,1)} %param.5, f32[8192]{0:T(1024)S(1)} %copy-done.1), kind=kLoop, calls=%fused_computation | loop fusion | flops 67108864 | bytes 201359360 | tf_op jit(solution)/shard_map/mul | solution.py:22
  558.1 26.1 %fusion.21 = bf16[8192,1544]{0,1:T(8,128)(2,1)} fusion(f32[8192,1544]{0,1:T(8,128)} %get-tuple-element.13, f32[8192]{0:T(1024)S(1)} %broadcast_divide_fusion, f32[8192]{0:T(1024)S(1)} %bitcast.11, s32[8192]{0:T(1024)S(1)} %copy-done.2, f32[8192]{0:T(1024)S(1)} %pmax.7, s32[1544]{0:T(1024)S(1)} %copy-done.4), kind=kLoop, calls=%fused_computation.9.clone.clone.2 | loop fusion | flops 88539136 | bytes 76027936 | tf_op jit(solution)/shard_map/tv,td->vd/dot_general | solution.py:40
  584.2 123.9 %fusion.6 = f32[1544,4096]{1,0:T(8,128)} fusion(f32[4096]{0:T(1024)S(1)} %copy-done.6, bf16[8192,4096]{1,0:T(8,128)(2,1)} %param.5, f32[8192]{0:T(1024)S(1)} %copy-done.1, bf16[8192,1544]{0,1:T(8,128)(2,1)} %fusion.21), kind=kOutput, calls=%fused_computation.14 | convolution fusion | flops 103756627968 | bytes 117751808 | tf_op jit(solution)/shard_map/tv,td->vd/dot_general | solution.py:40
  708.0 1179.7 %reduce-scatter.5.cloned.1.call-done = f32[256,4096]{1,0:T(8,128)} async-done(((f32[8192,4096]{1,0:T(8,128)}), f32[256,4096]{1,0:T(8,128)}) %reduce-scatter.5.cloned.1.call-update) | async-done | bytes 4194320
  1887.7 4.7 multiply_reduce_fusion
  1892.4 46.9 %psum.15 = f32[4096]{0:T(1024)} all-reduce(f32[4096]{0:T(1024)S(1)} %get-tuple-element.4), channel_id=1, replica_groups=mesh['vp'=32] {'vp'}, use_global_device_ids=true, to_apply=%region_11.12 | all-reduce | flops 4096 | bytes 32768 | tf_op jit(solution)/shard_map/psum | solution.py:44
  1939.3 6.8 subtract_multiply_fusion
  (10 shorter events, 0.0 us)
Async XLA Ops:
  7.2 21.6 %copy-start.5 = (f32[4096]{0:T(1024)S(1)}, f32[4096]{0:T(1024)}, u32[]{:S(2)}) copy-start(f32[4096]{0:T(1024)} %param.8) | copy-start | bytes 49156
  7.2 336.0 %all-reduce.3.cloned.1.call-start = ((), (), s32[]{:S(2)}) async-start(), calls=%async_computation.1 | async-start | bytes 131072 | tf_op jit(solution)/shard_map/psum | solution.py:31
  28.8 121.2 %copy-start = (f32[8192]{0:T(1024)}, f32[8192]{0:T(1024)S(1)}, u32[]{:S(2)}) copy-start(f32[8192]{0:T(1024)S(1)} %add_rsqrt_fusion) | copy-start | bytes 98308
  28.8 163.2 %copy-start.2 = (s32[8192]{0:T(1024)S(1)}, s32[8192]{0:T(1024)}, u32[]{:S(2)}) copy-start(s32[8192]{0:T(1024)} %param.6) | copy-start | bytes 98308
  28.8 163.2 %copy-start.4 = (s32[1544]{0:T(1024)S(1)}, s32[1544]{0:T(1024)}, u32[]{:S(2)}) copy-start(s32[1544]{0:T(1024)} %iota_add_fusion) | copy-start | bytes 18532
  150.0 194.1 %copy-start.3 = (f32[8192]{0:T(1024)S(1)}, f32[8192]{0:T(1024)}, u32[]{:S(2)}) copy-start(f32[8192]{0:T(1024)} %param.7) | copy-start | bytes 98308
  215.7 1672.0 %reduce-scatter.5.cloned.1.call-start = ((), (), s32[]{:S(2)}) async-start(), calls=%async_computation.2 | async-start | bytes 138412032
  489.2 0.8 copy-start.1
  556.7 27.4 %copy-start.6 = (f32[4096]{0:T(1024)S(1)}, f32[4096]{0:T(1024)}, u32[]{:S(2)}) copy-start(f32[4096]{0:T(1024)} %param.8) | copy-start | bytes 49156
  584.1 1355.1 %copy-start.7 = (f32[256]{0:T(256)S(1)}, f32[256]{0:T(256)}, u32[]{:S(2)}) copy-start(f32[256]{0:T(256)} %dynamic-slice.3) | copy-start | bytes 3076
Sparse Core Ops, SparseCore 0:
  215.8 127.2 all-reduce.2
  489.4 1398.3 reduce-scatter.4
where the time goes:
time: 1950 us
  waiting for transfers between devices  1310 us (67%)
  matrix products  389 us (20%)
  other arithmetic  150 us (8%)
  blocking collectives  88.9 us (5%)
    unnamed x3, waiting for transfers between devices  1180 us
    dot_general x1, matrix products, local_step(): jnp.dot(d_logits, table_shard, preferred_element_type=jnp.float32)  144 us
    psum x1, waiting for transfers between devices, local_step(): row_stats = lax.psum(part_stats, vp_axis)  127 us
    dot_general x1, matrix products, local_step(): jnp.einsum('tv,td->vd', d_logits, hidden, preferred_element_type=jnp.floa...  124 us
    dot_general x1, matrix products, local_step(): jnp.einsum('td,vd->tv', hidden, table_shard, preferred_element_type=jnp.f...  121 us
    mul x1, other arithmetic, local_step(): x_hat = x_f32 * inv_rms  66.1 us
    psum x1, blocking collectives, local_step(): d_gain = lax.psum(jnp.sum(d_hidden * x_hat_loc, axis=0), vp_axis)  46.9 us
    pmax x1, blocking collectives, local_step(): row_max = lax.pmax(jnp.max(logits, axis=-1), vp_axis)  42 us
  transfers between devices with their start and end apart: 2, of which 2 were waited for; matrix products, arithmetic and copies ran while one was open for 11% of the time, Pallas kernels for 0%

commit v1 on v0

v1 whole, which is shorter than its diff:
```python
import functools

import jax
import jax.numpy as jnp
from jax import lax
from jax.experimental import pallas as pl
from jax.experimental.pallas import tpu as pltpu
from jax.sharding import PartitionSpec as P

VOCAB_REAL = 49155
LOGIT_SCALE = 6.0
NORM_EPS = 1e-6
MESH = pl.DeviceIdType.MESH

GROUP = 8
ROWS = 32 * GROUP
COL_A, COL_B, COL_C = 896, 1792, 1408
DEPTH = 6


def step_kernel(
    n_chunks, res, lab, wgt, gain, tab,
    dx_out, de_out, dg_out, loss_out,
    ev, h, zt, dzt, dz, acc, op, r0,
    r1a, r1b, r1c, r2c, zra, zla, zrb, zlb, zrc, zlc,
    fsa, fka, r3a, fsb, fkb, r3b,
    st, tacc, ssq, dhf, xr, dxb, dgacc, dg1, dg2,
    sem_in, sem_out, sem_p, cred, nbr, sem_st, sem_g1, sem_g2,
    sem_a, sem_b, sem_c,
):
    vocab, width = ev.shape
    edges = list(range(0, max(vocab - 511, 1), 512)) + [vocab]
    blocks = [(a, b - a) for a, b in zip(edges, edges[1:])]
    me = lax.axis_index("vp")
    c, x, y, z = me % 2, (me // 2) % 2, (me // 4) % 2, me // 8

    def dev(zz, yy, xx, cc):
        return (((zz * 2 + yy) * 2 + xx) * 2 + cc,)

    def send(src, dst, ssem, rsem, to):
        return pltpu.make_async_remote_copy(src, dst, ssem, rsem, device_id=to, device_id_type=MESH)

    nbr_x, nbr_y = dev(z, y, 1 - x, c), dev(z, 1 - y, x, c)
    nbr_r, nbr_l = dev(z + 1, y, x, c), dev(z - 1, y, x, c)
    partner = dev(z, y, x, 1 - c)

    def load_x(n, half):
        return pltpu.make_async_copy(res.at[:, half, n], h.at[n % 2, pl.ds(16 * half, 16)], sem_in.at[half])

    def load_own(n):
        return pltpu.make_async_copy(res.at[me // 2, me % 2, n], xr.at[n % 2], sem_in.at[2 + n % 2])

    def store_dx(n):
        return pltpu.make_async_copy(dxb.at[n % 2], dx_out.at[n], sem_out.at[n % 2])

    def norm(n):
        slot = n % 2
        g = gain[...]

        def squares(i, _):
            xt = h[slot, i].astype(jnp.float32)
            sq = xt * xt
            ssq[i] = sum(sq[:, j : j + 128] for j in range(0, width, 128))
            return 0

        def scale(i, _):
            inv = ssq[i][:, 0:1]
            xt = h[slot, i].astype(jnp.float32)
            h[slot, i] = ((xt * inv) * g).astype(jnp.bfloat16)
            return 0

        lax.fori_loop(0, 32, squares, 0, unroll=4)
        mean = jnp.sum(ssq[...], axis=-1, keepdims=True) * (1.0 / width)
        ssq[...] = jnp.broadcast_to(lax.rsqrt(mean + NORM_EPS), ssq.shape)
        lax.fori_loop(0, 32, scale, 0, unroll=4)

    def logits(n):
        top = jnp.full((1, ROWS), -jnp.inf, jnp.float32)
        hn = h[n % 2].reshape(ROWS, width)
        for a, m in blocks:
            t = lax.dot_general(ev[a : a + m, :], hn, (((1,), (1,)), ((), ())), preferred_element_type=jnp.float32)
            t = t / LOGIT_SCALE
            ids = me * vocab + a + lax.broadcasted_iota(jnp.int32, (m, ROWS), 0)
            t = jnp.where(ids < VOCAB_REAL, t, -jnp.inf)
            zt[a : a + m, :] = t
            top = jnp.maximum(top, jnp.max(t, axis=0, keepdims=True))
        return top

    full_tiles = vocab // 128
    tail = vocab - full_tiles * 128

    def local_lse(n, top):
        lb = lab[pl.ds(n, 1), :] - me * vocab

        def part(a, m, s, t):
            v = zt[pl.ds(a, m), :]
            ids = a + lax.broadcasted_iota(jnp.int32, (m, ROWS), 0)
            e = jnp.exp(v - top).reshape(m // 8, 8, ROWS)
            hit = jnp.where(ids == lb, v, 0.0).reshape(m // 8, 8, ROWS)
            return s + jnp.sum(e, axis=0), t + jnp.sum(hit, axis=0)

        zero = jnp.zeros((8, ROWS), jnp.float32)
        s, t = lax.fori_loop(0, full_tiles, lambda i, v: part(pl.multiple_of(i * 128, 128), 128, *v), (zero, zero))
        s, t = part(full_tiles * 128, tail, s, t)
        tacc[1:2, :] += wgt[pl.ds(n, 1), :] * jnp.sum(t, axis=0, keepdims=True)
        return top + jnp.log(jnp.sum(s, axis=0, keepdims=True))

    def merge(ref, slot, count):
        rows = [ref[slot, q] for q in range(count)]
        top = functools.reduce(jnp.maximum, rows)
        return top + jnp.log(sum(jnp.exp(r - top) for r in rows))

    def grad_logits(k, lse):
        lb = lab[pl.ds(k, 1), :] - me * vocab
        w = wgt[pl.ds(k, 1), :]
        for a, m in [(i * 128, 128) for i in range(full_tiles)] + [(full_tiles * 128, tail)]:
            ids = a + lax.broadcasted_iota(jnp.int32, (m, ROWS), 0)
            p = jnp.exp(zt[a : a + m, :] - lse)
            d = (jnp.where(ids == lb, p - 1.0, p) * w).astype(jnp.bfloat16)
            dzt[a : a + m, :] = d
            dz[:, a : a + m] = d.T

    def embed_grad(k):
        tile = width // 4
        for a, m in blocks:
            for j in range(4):
                cols = pl.ds(j * tile, tile)
                acc[a : a + m, cols] += jnp.dot(dzt[a : a + m, :], h[k % 2, :, :, cols].reshape(ROWS, tile), preferred_element_type=jnp.float32)

    def send_p(half):
        cols = pl.ds(half * (width // 2), width // 2)
        return send(op.at[2, :, :, :, :, cols], r0.at[:, :, :, :, cols], sem_p.at[0, half], sem_p.at[1, half], partner)

    def hidden_grad(k):
        own = k % 2
        eq0 = 1 - c
        where = (eq0 * own + (1 - eq0) * 2, c * own + (1 - c) * 2)
        for half in range(2):
            cols = pl.ds(half * (width // 2), width // 2)
            r = jnp.dot(dz[...], ev[:, cols], preferred_element_type=jnp.float32)
            for q in range(2):
                op[where[q], :, :, :, :, cols] = r[q * 128 : (q + 1) * 128].reshape(4, 2, 2, 8, width // 2)
            if half == 0:
                @pl.when(k >= 1)
                def _():
                    pl.semaphore_wait(cred, 1)
            send_p(half).start()

    def add_partner(k):
        for half in range(2):
            send_p(half).wait()

        def body(i, _):
            op[k % 2, i] += r0[i]
            return 0

        lax.fori_loop(0, 4, body, 0)

        @pl.when(k < n_chunks - 1)
        def _():
            pl.semaphore_signal(cred, 1, device_id=partner, device_id_type=MESH)

    def swap8(buf, slot, sem):
        out = []
        for q in range(1, 8):
            qy, qx, qc = q // 4, (q // 2) % 2, q % 2
            to = dev(z, y + qy * (1 - 2 * y), x + qx * (1 - 2 * x), c + qc * (1 - 2 * c))
            out.append(send(buf.at[slot, 0], buf.at[slot, q], sem.at[0, slot, q], sem.at[1, slot, q], to))
        return out

    def swap32(buf, slot, sem):
        out = []
        for q in range(1, 32):
            qz, qy, qx, qc = q // 8, (q // 4) % 2, (q // 2) % 2, q % 2
            to = dev((z + qz) % 4, y + qy * (1 - 2 * y), x + qx * (1 - 2 * x), c + qc * (1 - 2 * c))
            there = ((4 - qz) % 4) * 8 + q % 8
            out.append(send(buf.at[slot, 0], buf.at[slot, there], sem.at[0, slot, q], sem.at[1, slot, there], to))
        return out

    def swap4(buf, slot, sem):
        out = []
        for q in range(1, 4):
            out.append(send(buf.at[slot, 0], buf.at[slot, 4 - q], sem.at[0, slot, q], sem.at[1, slot, 4 - q], dev((z + q) % 4, y, x, c)))
        return out

    def start(copies):
        for cp in copies:
            cp.start()

    def wait(copies):
        for cp in copies:
            cp.wait_send()
        for cp in copies:
            cp.wait_recv()

    def z_copies(zr, zl, s1, sl, t, zslot, sem, par):
        sl_z = zslot[t]
        sl_p = zslot[t - 1] if t else 0
        right = {
            "send": (z <= min(t, 2)),
            "recv": (z >= 1) & (z <= t + 1),
            "first": send(s1.at[sl, 3 - t], zr.at[t, sl_z], sem.at[0, 0, t, par], sem.at[1, 0, t, par], nbr_r),
        }
        left = {
            "send": (z >= 3 - t) & (z >= 1),
            "recv": (z <= 2) & (z >= 2 - t),
            "first": send(s1.at[sl, t], zl.at[t, sl_z], sem.at[0, 1, t, par], sem.at[1, 1, t, par], nbr_l),
        }
        if t:
            right["next"] = send(zr.at[t - 1, sl_p], zr.at[t, sl_z], sem.at[0, 0, t, par], sem.at[1, 0, t, par], nbr_r)
            left["next"] = send(zl.at[t - 1, sl_p], zl.at[t, sl_z], sem.at[0, 1, t, par], sem.at[1, 1, t, par], nbr_l)
        return right, left

    def z_wait(right, left):
        for way in (right, left):
            @pl.when(way["send"])
            def _(way=way):
                way["first"].wait_send()

            @pl.when(way["recv"])
            def _(way=way):
                way["first"].wait_recv()

    def z_start(right, left, zr, zl, s1, sl, t, zslot):
        sl_p = zslot[t - 1] if t else 0

        @pl.when(z == 0)
        def _():
            right["first"].start()

        @pl.when(z == 3)
        def _():
            left["first"].start()

        if t:
            @pl.when((z >= 1) & right["send"])
            def _():
                zr[t - 1, sl_p] += s1[sl, 3 - t + z]
                right["next"].start()

            @pl.when((z <= 2) & left["send"])
            def _():
                zl[t - 1, sl_p] += s1[sl, t - (3 - z)]
                left["next"].start()

    def in_range(k):
        return (k >= 0) & (k < n_chunks)

    def serve_two(s, axis, col, size, r1, zr, zl, fs, fk, r3, sem1, semz, sem3):
        cols = pl.ds(col, size)
        first_nbr, last_nbr = (nbr_x, nbr_y) if axis == "x" else (nbr_y, nbr_x)
        q = y if axis == "x" else x

        def zs(k):
            return (k % 3, k % 3, k % 3)

        def copy1(k):
            src = op.at[k % 2, :, :, 1 - x, :, cols] if axis == "x" else op.at[k % 2, :, 1 - y, :, :, cols]
            return send(src, r1.at[k % 5], sem1.at[0, k % 2], sem1.at[1, k % 2], first_nbr)

        def copy3(k):
            return send(fs, r3.at[k % 2], sem3.at[0, k % 2], sem3.at[1, k % 2], last_nbr)

        def zc(k, t):
            return z_copies(zr, zl, r1, k % 5, t, zs(k), semz, k % 2)

        k = s - 6

        @pl.when(in_range(k))
        def _():
            copy3(k).wait()
            dhf[:, cols] = fk[...] + r3[k % 2]

        k5 = s - 5

        @pl.when(in_range(k5))
        def _():
            z_wait(*zc(k5, 2))
            sl = k5 % 5
            fs[...] = r1[sl, z, 1 - q]
            fk[...] = r1[sl, z, q]

            @pl.when(z >= 1)
            def _():
                fs[...] += zr[2, k5 % 3, 1 - q]
                fk[...] += zr[2, k5 % 3, q]

            @pl.when(z <= 2)
            def _():
                fs[...] += zl[2, k5 % 3, 1 - q]
                fk[...] += zl[2, k5 % 3, q]

            copy3(k5).start()

        for t, back in ((2, 4), (1, 3)):
            kt = s - back

            @pl.when(in_range(kt))
            def _(kt=kt, t=t):
                z_wait(*zc(kt, t - 1))
                z_start(*zc(kt, t), zr, zl, r1, kt % 5, t, zs(kt))

        k2 = s - 2

        @pl.when(in_range(k2))
        def _():
            copy1(k2).wait()
            for b in range(4):
                kept = op[k2 % 2, b, :, x, :, cols] if axis == "x" else op[k2 % 2, b, y, :, :, cols]
                r1[k2 % 5, b] += kept
            z_start(*zc(k2, 0), zr, zl, r1, k2 % 5, 0, zs(k2))

        k1 = s - 1

        @pl.when(in_range(k1))
        def _():
            copy1(k1).start()

    def serve_c(s):
        cols = pl.ds(COL_A + COL_B, COL_C)

        def zs(k):
            return (k % 3, k % 3, k % 3)

        def copy1(k):
            return send(op.at[k % 2, :, :, 1 - x, :, cols], r1c.at[k % 3], sem_c["1"].at[0, k % 2], sem_c["1"].at[1, k % 2], nbr_x)

        def copy2(k):
            return send(r1c.at[k % 3, :, 1 - y], r2c.at[k % 5], sem_c["2"].at[0, k % 2], sem_c["2"].at[1, k % 2], nbr_y)

        def zc(k, t):
            return z_copies(zrc, zlc, r2c, k % 5, t, zs(k), sem_c["z"], k % 2)

        k = s - 6

        @pl.when(in_range(k))
        def _():
            z_wait(*zc(k, 2))
            dhf[:, cols] = r2c[k % 5, z]

            @pl.when(z >= 1)
            def _():
                dhf[:, cols] += zrc[2, k % 3]

            @pl.when(z <= 2)
            def _():
                dhf[:, cols] += zlc[2, k % 3]

        for t, back in ((2, 5), (1, 4)):
            kt = s - back

            @pl.when(in_range(kt))
            def _(kt=kt, t=t):
                z_wait(*zc(kt, t - 1))
                z_start(*zc(kt, t), zrc, zlc, r2c, kt % 5, t, zs(kt))

        k3 = s - 3

        @pl.when(in_range(k3))
        def _():
            copy2(k3).wait()
            for b in range(4):
                r2c[k3 % 5, b] += r1c[k3 % 3, b, y]
            z_start(*zc(k3, 0), zrc, zlc, r2c, k3 % 5, 0, zs(k3))

        k2 = s - 2

        @pl.when(in_range(k2))
        def _():
            copy1(k2).wait()
            for b in range(4):
                r1c[k2 % 3, b] += op[k2 % 2, b, :, x, :, cols]
            copy2(k2).start()

        k1 = s - 1

        @pl.when(in_range(k1))
        def _():
            copy1(k1).start()

    def finish(k):
        load_own(k).wait()

        @pl.when(k >= 2)
        def _():
            store_dx(k - 2).wait()

        xo = xr[k % 2].astype(jnp.float32)
        inv = lax.rsqrt(jnp.mean(xo * xo, axis=-1, keepdims=True) + NORM_EPS)
        xh = xo * inv
        dh = dhf[...] / LOGIT_SCALE
        dgacc[...] += dh * xh
        u = dh * gain[...]
        dxb[k % 2] = inv * (u - xh * jnp.mean(u * xh, axis=-1, keepdims=True))
        store_dx(k).start()

    def tell_neighbours():
        pl.semaphore_signal(nbr.at[0], 1, device_id=nbr_x, device_id_type=MESH)
        pl.semaphore_signal(nbr.at[1], 1, device_id=nbr_y, device_id_type=MESH)

        @pl.when(z <= 2)
        def _():
            pl.semaphore_signal(nbr.at[2], 1, device_id=nbr_r, device_id_type=MESH)

        @pl.when(z >= 1)
        def _():
            pl.semaphore_signal(nbr.at[3], 1, device_id=nbr_l, device_id_type=MESH)

    def hear_neighbours():
        pl.semaphore_wait(nbr.at[0], 1)
        pl.semaphore_wait(nbr.at[1], 1)

        @pl.when(z >= 1)
        def _():
            pl.semaphore_wait(nbr.at[2], 1)

        @pl.when(z <= 2)
        def _():
            pl.semaphore_wait(nbr.at[3], 1)

    get_tab = pltpu.make_async_copy(tab, ev, sem_in.at[4])
    get_tab.start()
    for half in range(2):
        load_x(0, half).start()
    acc[...] = jnp.zeros_like(acc)
    tacc[...] = jnp.zeros_like(tacc)
    dgacc[...] = jnp.zeros_like(dgacc)
    get_tab.wait()
    last = n_chunks + DEPTH

    def iteration(i, _):
        s = i - 1
        busy = in_range(s)
        ahead = i < n_chunks
        scope = jax.named_scope

        with scope("stat"):
            @pl.when(busy)
            def _():
                wait(swap32(st, s % 2, sem_st))

        with scope("dz"):
            @pl.when(busy)
            def _():
                lse = merge(st, s % 2, 32)
                tacc[0:1, :] += wgt[pl.ds(s, 1), :] * lse
                grad_logits(s, lse)

        with scope("xwait"):
            @pl.when(ahead)
            def _():
                for half in range(2):
                    load_x(i, half).wait()

        with scope("norm"):
            @pl.when(ahead)
            def _():
                norm(i)

        with scope("logits"):
            @pl.when(ahead)
            def _():
                top = logits(i)
                st[i % 2, 0] = local_lse(i, top)

        with scope("hear"):
            @pl.when(ahead)
            def _():
                start(swap32(st, i % 2, sem_st))

            @pl.when(i >= 2)
            def _():
                hear_neighbours()

        with scope("partner"):
            @pl.when(in_range(s - 1))
            def _():
                add_partner(s - 1)

        with scope("serve_a"):
            serve_two(s, "x", 0, COL_A, r1a, zra, zla, fsa, fka, r3a, sem_a["1"], sem_a["z"], sem_a["3"])

        with scope("serve_b"):
            serve_two(s, "y", COL_A, COL_B, r1b, zrb, zlb, fsb, fkb, r3b, sem_b["1"], sem_b["z"], sem_b["3"])

        with scope("serve_c"):
            serve_c(s)

        with scope("tell"):
            @pl.when((i >= 1) & (i < last))
            def _():
                tell_neighbours()

        with scope("finish"):
            k = s - 5

            @pl.when(in_range(k))
            def _():
                load_own(k).start()

            @pl.when(in_range(k - 1))
            def _():
                finish(k - 1)

        with scope("de"):
            @pl.when(busy & (s < n_chunks - 1))
            def _():
                embed_grad(s)

            @pl.when(i + 1 < n_chunks)
            def _():
                for half in range(2):
                    load_x(i + 1, half).start()

        with scope("dh"):
            @pl.when(busy)
            def _():
                hidden_grad(s)

        with scope("de_last"):
            @pl.when(s == n_chunks - 1)
            def _():
                embed_grad(s)

        with scope("store"):
            @pl.when(i == n_chunks)
            def _():
                pltpu.make_async_copy(acc, de_out, sem_out.at[2]).start()

        return 0

    lax.fori_loop(0, last + 1, iteration, 0)
    dg1[0, 0, :, 0:width] = jnp.sum(dgacc[...], axis=0, keepdims=True)
    dg1[0, 0, :, width : width + ROWS] = tacc[1:2, :]
    start(swap8(dg1, 0, sem_g1))
    wait(swap8(dg1, 0, sem_g1))
    dg2[0, 0] = sum(dg1[0, q] for q in range(8))
    start(swap4(dg2, 0, sem_g2))
    wait(swap4(dg2, 0, sem_g2))
    total = sum(dg2[0, q] for q in range(4))
    dg_out[...] = total[:, 0:width]
    loss_out[...] = tacc[0:1, :] - total[:, width : width + ROWS]
    for n in (n_chunks - 2, n_chunks - 1):
        store_dx(n).wait()
    pltpu.make_async_copy(acc, de_out, sem_out.at[2]).wait()


def solution(mesh):
    def local_step(residual, labels, loss_mask, norm_gain, table_shard):
        tokens, width = residual.shape
        vocab = table_shard.shape[0]
        n_chunks = tokens // ROWS
        f32, bf16 = jnp.float32, jnp.bfloat16

        def by_chunk(v):
            return v.reshape(16, 2, n_chunks, GROUP).transpose(2, 1, 0, 3).reshape(n_chunks, ROWS)

        weight = loss_mask / jnp.sum(loss_mask)
        dma = pltpu.SemaphoreType.DMA
        vm = pltpu.VMEM
        scratch = [
            vm((vocab, width), bf16), vm((2, 32, GROUP, width), bf16),
            vm((vocab, ROWS), f32), vm((vocab, ROWS), bf16), vm((ROWS, vocab), bf16),
            vm((vocab, width), f32), vm((3, 4, 2, 2, 8, width), f32), vm((4, 2, 2, 8, width), f32),
            vm((5, 4, 2, 8, COL_A), f32), vm((5, 4, 2, 8, COL_B), f32),
            vm((3, 4, 2, 8, COL_C), f32), vm((5, 4, 8, COL_C), f32),
            vm((3, 3, 2, 8, COL_A), f32), vm((3, 3, 2, 8, COL_A), f32),
            vm((3, 3, 2, 8, COL_B), f32), vm((3, 3, 2, 8, COL_B), f32),
            vm((3, 3, 8, COL_C), f32), vm((3, 3, 8, COL_C), f32),
            vm((8, COL_A), f32), vm((8, COL_A), f32), vm((2, 8, COL_A), f32),
            vm((8, COL_B), f32), vm((8, COL_B), f32), vm((2, 8, COL_B), f32),
            vm((2, 32, 1, ROWS), f32), vm((8, ROWS), f32), vm((32, 8, 128), f32),
            vm((8, width), f32), vm((2, 8, width), bf16), vm((2, 8, width), f32), vm((8, width), f32),
            vm((1, 8, 1, width + ROWS), f32), vm((1, 4, 1, width + ROWS), f32),
            dma((5,)), dma((3,)), dma((2, 2)), pltpu.SemaphoreType.REGULAR, pltpu.SemaphoreType.REGULAR((4,)),
            dma((2, 2, 32)), dma((2, 1, 8)), dma((2, 1, 4)),
            {"1": dma((2, 2)), "z": dma((2, 2, 3, 2)), "3": dma((2, 2))},
            {"1": dma((2, 2)), "z": dma((2, 2, 3, 2)), "3": dma((2, 2))},
            {"1": dma((2, 2)), "z": dma((2, 2, 3, 2)), "2": dma((2, 2))},
        ]
        whole = pl.BlockSpec(memory_space=pltpu.VMEM)
        raw = pl.BlockSpec(memory_space=pl.ANY)
        dx, de, dg, loss = pl.pallas_call(
            functools.partial(step_kernel, n_chunks),
            out_shape=(
                jax.ShapeDtypeStruct((n_chunks, GROUP, width), f32),
                jax.ShapeDtypeStruct((vocab, width), f32),
                jax.ShapeDtypeStruct((1, width), f32),
                jax.ShapeDtypeStruct((1, ROWS), f32),
            ),
            in_specs=[raw, whole, whole, whole, raw],
            out_specs=(raw, raw, whole, whole),
            scratch_shapes=scratch,
            compiler_params=pltpu.CompilerParams(vmem_limit_bytes=67043328, has_side_effects=True),
            name="head_step",
        )(
            residual.reshape(16, 2, n_chunks, GROUP, width),
            by_chunk(labels),
            by_chunk(weight),
            norm_gain.reshape(1, width),
            table_shard,
        )
        return jnp.sum(loss), dx.reshape(n_chunks * GROUP, width), de / LOGIT_SCALE, dg.reshape(width)

    return jax.shard_map(local_step, mesh=mesh, in_specs=(P(), P(), P(), P(), P("vp", None)), out_specs=(P(), P("vp", None), P("vp", None), P()), check_vma=False)
```

time: 1950 us -> 611 us (0.31)
  waiting for transfers between devices: 1310 us -> 0 us
  Pallas kernels: 0 us -> 581 us
  matrix products: 389 us -> 0 us
  other arithmetic: 150 us -> 23 us
  blocking collectives: 88.9 us -> 0 us
    unnamed x3 -> x0, waiting for transfers between devices: 1180 us -> none
    pallas_call x0 -> x1, Pallas kernels: none -> 581 us  [local_step(): pl.pallas_call(functools.partial(step_kernel, n_chunks), out_shape=(jax.S...]
    dot_general x3 -> x0, matrix products: 389 us -> none  [the longest x1 144 us: local_step(): jnp.dot(d_logits, table_shard, preferred_element_type=jnp.float32)]
    psum x1 -> x0, waiting for transfers between devices: 127 us -> none  [local_step(): row_stats = lax.psum(part_stats, vp_axis)]
    mul x2 -> x0, other arithmetic: 72.9 us -> none  [the longest x1 66.1 us: local_step(): x_hat = x_f32 * inv_rms]
    psum x1 -> x0, blocking collectives: 46.9 us -> none  [local_step(): d_gain = lax.psum(jnp.sum(d_hidden * x_hat_loc, axis=0), vp_axis)]
    reduce_sum x4 -> x2, other arithmetic: 49.1 us -> 2.59 us  [the longest x1 1.37 us: local_step(): weight = loss_mask / jnp.sum(loss_mask)]
    pmax x1 -> x0, blocking collectives: 42 us -> none  [local_step(): row_max = lax.pmax(jnp.max(logits, axis=-1), vp_axis)]
  transfers between devices with their start and end apart: 2 -> 0, of which waited for: 2 -> 0; matrix products, arithmetic and copies ran while one was open for 11% -> 0% of each run, Pallas kernels for 0% -> 0%
where the time goes in v1:
time: 611 us; the launch traced here: 610 us
  Pallas kernels  581 us (95%)
  other arithmetic  23 us (4%)
    pallas_call x1, Pallas kernels, local_step(): pl.pallas_call(functools.partial(step_kernel, n_chunks), out_shape=(jax.S...  581 us
    div x1, other arithmetic, local_step(): de / LOGIT_SCALE  19 us

profile of v1, /device:TPU:0, one launch (start us, length us, event | category | flops | bytes accessed | tf_op | source)
XLA Modules:
  0.0 610.4 jit_solution(11825286120927043468)
XLA Ops:
  0.6 1.4 reduce_sum.18
  2.0 1.4 broadcast_divide_fusion
  3.4 0.3 reshape.35
  3.7 0.2 copy.10
  3.9 0.7 copy.12.wgt
  4.6 1.0 reshape.33
  5.7 0.2 copy.9
  5.9 0.7 copy.11.lab
  6.6 581.0 %head_step.1 = (f32[32,8,4096]{2,1,0:T(8,128)}, f32[1544,4096]{1,0:T(8,128)}, f32[1,4096]{1,0:T(1,128)}, f32[1,256]{1,0:T(1,128)}) custom-call(bf16[16,2,32,8,4096]{4,3,2,1,0:T(8,128)(2,1)} %bitcast.res, s32[32,256]{1,0:T(8,128)} %copy.11.lab, f32[32,256]{1,0:T(8,128)} %copy.12.wgt, f32[1,4096]{1,0:T(1,128)} %bitcast.14, bf16[1544,4096]{1,0:T(8,128)(2,1)} %tab.1), custom_call_target="tpu_custom_call" | custom-call | tf_op jit(solution)/shard_map/head_step/pallas_call | solution.py:583
  587.6 1.2 reduce_sum.19
  588.8 0.0 copy-start
  588.8 0.0 copy-start.1
  588.8 19.0 %broadcast_multiply_fusion = f32[1544,4096]{1,0:T(8,128)} fusion(f32[1544,4096]{1,0:T(8,128)} %get-tuple-element.10), kind=kLoop, calls=%fused_computation | loop fusion | flops 6324224 | bytes 50593792 | tf_op jit(solution)/shard_map/div | solution.py:603
  607.8 0.0 copy-done
  607.8 2.0 copy.15
  609.8 0.0 copy-done.1
  609.8 0.6 copy.16
Async XLA Ops:
  588.8 19.0 %copy-start = (f32[32,8,4096]{2,1,0:T(8,128)S(1)}, f32[32,8,4096]{2,1,0:T(8,128)}, u32[]{:S(2)}) copy-start(f32[32,8,4096]{2,1,0:T(8,128)} %get-tuple-element.9) | copy-start | bytes 12582916
  588.8 21.0 %copy-start.1 = (f32[1,4096]{1,0:T(1,128)S(1)}, f32[1,4096]{1,0:T(1,128)}, u32[]{:S(2)}) copy-start(f32[1,4096]{1,0:T(1,128)} %get-tuple-element.11) | copy-start | bytes 49156

commit v2 on v1

v2 whole, which is shorter than its diff:
```python
import functools

import jax
import jax.numpy as jnp
from jax import lax
from jax.experimental import pallas as pl
from jax.experimental.pallas import tpu as pltpu
from jax.sharding import PartitionSpec as P

VOCAB_REAL = 49155
LOGIT_SCALE = 6.0
NORM_EPS = 1e-6
MESH = pl.DeviceIdType.MESH

GROUP = 8
ROWS = 32 * GROUP
COL_A, COL_B, COL_C = 896, 1792, 1408
DEPTH = 6
VMEM_LIMIT = 67043328
GRID = (4, 2, 2)


def step_kernel(
    n_chunks, res, tok, gain, tab,
    dx_out, de_out, dg_out, loss_out,
    ev, h, zt, dzt, dz, acc, op, r0,
    r1a, r1b, r1c, r2c, zra, zla, zrb, zlb, zrc, zlc,
    fsa, fka, r3a, fsb, fkb, r3b,
    st, tacc, ssq, dhf, xr, dxb, dgacc, dg1, dg2,
    sem_in, sem_tab, sem_out, sem_p, cred, nbr, sem_st, sem_g1, sem_g2,
    sem_a, sem_b, sem_c,
):
    vocab, width = ev.shape
    edges = list(range(0, max(vocab - 511, 1), 512)) + [vocab]
    blocks = [(a, b - a) for a, b in zip(edges, edges[1:])]
    me = lax.axis_index("vp")
    c, x, y, z = me % 2, (me // 2) % 2, (me // 4) % 2, me // 8

    def dev(zz, yy, xx, cc):
        return (((zz * 2 + yy) * 2 + xx) * 2 + cc,)

    def send(src, dst, ssem, rsem, to):
        return pltpu.make_async_remote_copy(src, dst, ssem, rsem, device_id=to, device_id_type=MESH)

    def hop(src, dst, sem, k, to):
        return send(src, dst, sem.at[0, k % 2], sem.at[1, k % 2], to)

    nbr_x, nbr_y = dev(z, y, 1 - x, c), dev(z, 1 - y, x, c)
    nbr_r, nbr_l = dev(z + 1, y, x, c), dev(z - 1, y, x, c)
    partner = dev(z, y, x, 1 - c)

    def load_x(n, half):
        return pltpu.make_async_copy(res.at[:, half, n], h.at[n % 2, pl.ds(16 * half, 16)], sem_in.at[half])

    def tab_block(j):
        a, m = blocks[j]
        return pltpu.make_async_copy(tab.at[pl.ds(a, m)], ev.at[pl.ds(a, m)], sem_tab.at[j])

    def load_own(n):
        return pltpu.make_async_copy(res.at[me // 2, me % 2, n], xr.at[n % 2], sem_in.at[2 + n % 2])

    def store_dx(n):
        return pltpu.make_async_copy(dxb.at[n % 2], dx_out.at[n], sem_out.at[n % 2])

    def label_rows(n):
        return tok[0, pl.ds(n, 1), :].astype(jnp.int32) - me * vocab

    def weights(n):
        return tok[1, pl.ds(n, 1), :] / tacc[2:3, :]

    def norm(n):
        slot = n % 2
        pieces = range(0, width, 256)

        def piece(i, j):
            return h[slot, i, :, j : j + 256].astype(jnp.float32)

        def squares(i, _):
            parts = []
            for j in pieces:
                sq = piece(i, j)
                sq = sq * sq
                parts.append(sq[:, :128] + sq[:, 128:])
            while len(parts) > 1:
                parts = [p + q for p, q in zip(parts[::2], parts[1::2])]
            ssq[i] = parts[0]
            return 0

        def scale(i, _):
            inv = jnp.concatenate([ssq[i], ssq[i]], axis=1)
            for j in pieces:
                h[slot, i, :, j : j + 256] = ((piece(i, j) * inv) * gain[:, j : j + 256]).astype(jnp.bfloat16)
            return 0

        lax.fori_loop(0, 32, squares, 0, unroll=4)
        mean = jnp.sum(ssq[...], axis=-1, keepdims=True) * (1.0 / width)
        ssq[...] = jnp.broadcast_to(lax.rsqrt(mean + NORM_EPS), ssq.shape)
        lax.fori_loop(0, 32, scale, 0, unroll=4)

    def logits(n):
        top = jnp.full((1, ROWS), -jnp.inf, jnp.float32)
        hn = h[n % 2].reshape(ROWS, width)
        for a, m in blocks:
            t = lax.dot_general(ev[a : a + m, :], hn, (((1,), (1,)), ((), ())), preferred_element_type=jnp.float32)
            t = t * (1.0 / LOGIT_SCALE)
            ids = me * vocab + a + lax.broadcasted_iota(jnp.int32, (m, ROWS), 0)
            t = jnp.where(ids < VOCAB_REAL, t, -jnp.inf)
            zt[a : a + m, :] = t
            top = jnp.maximum(top, jnp.max(t, axis=0, keepdims=True))
        return top

    full_tiles = vocab // 128
    tail = vocab - full_tiles * 128

    def local_lse(n, top):
        lb = label_rows(n)

        def part(a, m, s, t):
            v = zt[pl.ds(a, m), :]
            ids = a + lax.broadcasted_iota(jnp.int32, (m, ROWS), 0)
            e = jnp.exp(v - top).reshape(m // 8, 8, ROWS)
            hit = jnp.where(ids == lb, v, 0.0).reshape(m // 8, 8, ROWS)
            return s + jnp.sum(e, axis=0), t + jnp.sum(hit, axis=0)

        zero = jnp.zeros((8, ROWS), jnp.float32)
        s, t = lax.fori_loop(0, full_tiles, lambda i, v: part(pl.multiple_of(i * 128, 128), 128, *v), (zero, zero))
        s, t = part(full_tiles * 128, tail, s, t)
        tacc[1:2, :] += weights(n) * jnp.sum(t, axis=0, keepdims=True)
        return top + jnp.log(jnp.sum(s, axis=0, keepdims=True))

    def merge(ref, slot, count):
        rows = [ref[slot, q] for q in range(count)]
        top = functools.reduce(jnp.maximum, rows)
        return top + jnp.log(sum(jnp.exp(r - top) for r in rows))

    def grad_logits(k, lse):
        lb = label_rows(k)
        w = weights(k)
        for a, m in [(i * 128, 128) for i in range(full_tiles)] + [(full_tiles * 128, tail)]:
            ids = a + lax.broadcasted_iota(jnp.int32, (m, ROWS), 0)
            p = jnp.exp(zt[a : a + m, :] - lse)
            d = (jnp.where(ids == lb, p - 1.0, p) * w).astype(jnp.bfloat16)
            dzt[a : a + m, :] = d
            dz[:, a : a + m] = d.T

    def embed_grad(k):
        tile = width // 4
        for a, m in blocks:
            for j in range(4):
                cols = pl.ds(j * tile, tile)
                acc[a : a + m, cols] += jnp.dot(dzt[a : a + m, :], h[k % 2, :, :, cols].reshape(ROWS, tile), preferred_element_type=jnp.float32)

    def send_p(half):
        cols = pl.ds(half * (width // 2), width // 2)
        return send(op.at[2, :, :, :, :, cols], r0.at[:, :, :, :, cols], sem_p.at[0, half], sem_p.at[1, half], partner)

    def hidden_grad(k):
        own = k % 2
        eq0 = 1 - c
        where = (eq0 * own + (1 - eq0) * 2, c * own + (1 - c) * 2)
        for half in range(2):
            cols = pl.ds(half * (width // 2), width // 2)
            r = jnp.dot(dz[...], ev[:, cols], preferred_element_type=jnp.float32)
            for q in range(2):
                op[where[q], :, :, :, :, cols] = r[q * 128 : (q + 1) * 128].reshape(4, 2, 2, 8, width // 2)
            if half == 0:
                @pl.when(k >= 1)
                def _():
                    pl.semaphore_wait(cred, 1)
            send_p(half).start()

    def add_partner(k):
        for half in range(2):
            send_p(half).wait()

        def body(i, _):
            op[k % 2, i] += r0[i]
            return 0

        lax.fori_loop(0, 4, body, 0)

        @pl.when(k < n_chunks - 1)
        def _():
            pl.semaphore_signal(cred, 1, device_id=partner, device_id_type=MESH)

    def peer(q):
        qy, qx, qc = (q // 4) % 2, (q // 2) % 2, q % 2
        return dev((z + q // 8) % 4, y + qy * (1 - 2 * y), x + qx * (1 - 2 * x), c + qc * (1 - 2 * c))

    def swap8(buf, slot, sem):
        return [send(buf.at[slot, 0], buf.at[slot, q], sem.at[0, slot, q], sem.at[1, slot, q], peer(q)) for q in range(1, 8)]

    def swap32(buf, slot, sem):
        out = []
        for q in range(1, 32):
            there = ((4 - q // 8) % 4) * 8 + q % 8
            out.append(send(buf.at[slot, 0], buf.at[slot, there], sem.at[0, slot, q], sem.at[1, slot, there], peer(q)))
        return out

    def swap4(buf, slot, sem):
        return [
            send(buf.at[slot, 0], buf.at[slot, 4 - q], sem.at[0, slot, q], sem.at[1, slot, 4 - q], peer(8 * q))
            for q in range(1, 4)
        ]

    def start(copies):
        for cp in copies:
            cp.start()

    def wait(copies):
        for cp in copies:
            cp.wait_send()
        for cp in copies:
            cp.wait_recv()

    def z_copies(zr, zl, s1, sl, t, zslot, sem, par):
        ways = []
        for way, (buf, to, block) in enumerate(((zr, nbr_r, 3 - t), (zl, nbr_l, t))):
            sems = (sem.at[0, way, t, par], sem.at[1, way, t, par])
            first = send(s1.at[sl, block], buf.at[t, zslot], *sems, to)
            later = send(buf.at[t - 1, zslot], buf.at[t, zslot], *sems, to) if t else None
            behind, ahead = (z, 3 - z) if way == 0 else (3 - z, z)
            ways.append((behind, ahead, first, later))
        return ways

    def z_wait(ways, t):
        for behind, ahead, first, _ in ways:
            @pl.when((behind <= t) & (ahead > 0))
            def _(first=first):
                first.wait_send()

            @pl.when((behind > 0) & (behind <= t + 1))
            def _(first=first):
                first.wait_recv()

    def z_start(ways, zr, zl, s1, sl, t, zslot):
        for (behind, ahead, first, later), buf, block in zip(ways, (zr, zl), (3 - t + z, t - 3 + z)):
            @pl.when(behind == 0)
            def _(first=first):
                first.start()

            if t:
                @pl.when((behind > 0) & (behind <= t) & (ahead > 0))
                def _(buf=buf, block=block, later=later):
                    buf[t - 1, zslot] += s1[sl, block]
                    later.start()

    def in_range(k):
        return (k >= 0) & (k < n_chunks)

    def serve_two(s, axis, col, size, r1, zr, zl, fs, fk, r3, sem):
        cols = pl.ds(col, size)
        first_nbr, last_nbr = (nbr_x, nbr_y) if axis == "x" else (nbr_y, nbr_x)
        q = y if axis == "x" else x

        def copy1(k):
            src = op.at[k % 2, :, :, 1 - x, :, cols] if axis == "x" else op.at[k % 2, :, 1 - y, :, :, cols]
            return hop(src, r1.at[k % 5], sem["first"], k, first_nbr)

        def copy3(k):
            return hop(fs, r3.at[k % 2], sem["last"], k, last_nbr)

        def zc(k, t):
            return z_copies(zr, zl, r1, k % 5, t, k % 3, sem["z"], k % 2)

        k = s - 6

        @pl.when(in_range(k))
        def _():
            copy3(k).wait()
            dhf[:, cols] = fk[...] + r3[k % 2]

        k5 = s - 5

        @pl.when(in_range(k5))
        def _():
            z_wait(zc(k5, 2), 2)
            sl = k5 % 5
            fs[...] = r1[sl, z, 1 - q]
            fk[...] = r1[sl, z, q]

            @pl.when(z >= 1)
            def _():
                fs[...] += zr[2, k5 % 3, 1 - q]
                fk[...] += zr[2, k5 % 3, q]

            @pl.when(z <= 2)
            def _():
                fs[...] += zl[2, k5 % 3, 1 - q]
                fk[...] += zl[2, k5 % 3, q]

            copy3(k5).start()

        for t, back in ((2, 4), (1, 3)):
            kt = s - back

            @pl.when(in_range(kt))
            def _(kt=kt, t=t):
                z_wait(zc(kt, t - 1), t - 1)
                z_start(zc(kt, t), zr, zl, r1, kt % 5, t, kt % 3)

        k2 = s - 2

        @pl.when(in_range(k2))
        def _():
            copy1(k2).wait()
            for b in range(4):
                kept = op[k2 % 2, b, :, x, :, cols] if axis == "x" else op[k2 % 2, b, y, :, :, cols]
                r1[k2 % 5, b] += kept
            z_start(zc(k2, 0), zr, zl, r1, k2 % 5, 0, k2 % 3)

        k1 = s - 1

        @pl.when(in_range(k1))
        def _():
            copy1(k1).start()

    def serve_c(s):
        cols = pl.ds(COL_A + COL_B, COL_C)

        def copy1(k):
            return hop(op.at[k % 2, :, :, 1 - x, :, cols], r1c.at[k % 3], sem_c["first"], k, nbr_x)

        def copy2(k):
            return hop(r1c.at[k % 3, :, 1 - y], r2c.at[k % 5], sem_c["last"], k, nbr_y)

        def zc(k, t):
            return z_copies(zrc, zlc, r2c, k % 5, t, k % 3, sem_c["z"], k % 2)

        k = s - 6

        @pl.when(in_range(k))
        def _():
            z_wait(zc(k, 2), 2)
            dhf[:, cols] = r2c[k % 5, z]

            @pl.when(z >= 1)
            def _():
                dhf[:, cols] += zrc[2, k % 3]

            @pl.when(z <= 2)
            def _():
                dhf[:, cols] += zlc[2, k % 3]

        for t, back in ((2, 5), (1, 4)):
            kt = s - back

            @pl.when(in_range(kt))
            def _(kt=kt, t=t):
                z_wait(zc(kt, t - 1), t - 1)
                z_start(zc(kt, t), zrc, zlc, r2c, kt % 5, t, kt % 3)

        k3 = s - 3

        @pl.when(in_range(k3))
        def _():
            copy2(k3).wait()
            for b in range(4):
                r2c[k3 % 5, b] += r1c[k3 % 3, b, y]
            z_start(zc(k3, 0), zrc, zlc, r2c, k3 % 5, 0, k3 % 3)

        k2 = s - 2

        @pl.when(in_range(k2))
        def _():
            copy1(k2).wait()
            for b in range(4):
                r1c[k2 % 3, b] += op[k2 % 2, b, :, x, :, cols]
            copy2(k2).start()

        k1 = s - 1

        @pl.when(in_range(k1))
        def _():
            copy1(k1).start()

    def finish(k):
        load_own(k).wait()

        @pl.when(k >= 2)
        def _():
            store_dx(k - 2).wait()

        xo = xr[k % 2].astype(jnp.float32)
        inv = lax.rsqrt(jnp.mean(xo * xo, axis=-1, keepdims=True) + NORM_EPS)
        xh = xo * inv
        dh = dhf[...] / LOGIT_SCALE
        dgacc[...] += dh * xh
        u = dh * gain[...]
        dxb[k % 2] = inv * (u - xh * jnp.mean(u * xh, axis=-1, keepdims=True))
        store_dx(k).start()

    def tell_neighbours():
        pl.semaphore_signal(nbr.at[0], 1, device_id=nbr_x, device_id_type=MESH)
        pl.semaphore_signal(nbr.at[1], 1, device_id=nbr_y, device_id_type=MESH)

        @pl.when(z <= 2)
        def _():
            pl.semaphore_signal(nbr.at[2], 1, device_id=nbr_r, device_id_type=MESH)

        @pl.when(z >= 1)
        def _():
            pl.semaphore_signal(nbr.at[3], 1, device_id=nbr_l, device_id_type=MESH)

    def hear_neighbours():
        pl.semaphore_wait(nbr.at[0], 1)
        pl.semaphore_wait(nbr.at[1], 1)

        @pl.when(z >= 1)
        def _():
            pl.semaphore_wait(nbr.at[2], 1)

        @pl.when(z <= 2)
        def _():
            pl.semaphore_wait(nbr.at[3], 1)

    with jax.named_scope("init"):
        for half in range(2):
            load_x(0, half).start()
        for j in range(len(blocks)):
            tab_block(j).start()
        barrier = pltpu.get_barrier_semaphore()
        for q in range(1, 32):
            pl.semaphore_signal(barrier, 1, device_id=peer(q), device_id_type=MESH)
        tacc[...] = jnp.zeros_like(tacc)
        tacc[2:3, :] = jnp.broadcast_to(jnp.sum(tok[1], keepdims=True), (1, ROWS))
        dgacc[...] = jnp.zeros_like(dgacc)
    last = n_chunks + DEPTH

    def iteration(i, _):
        s = i - 1
        busy = in_range(s)
        ahead = i < n_chunks
        scope = jax.named_scope

        with scope("xwait"):
            @pl.when(ahead)
            def _():
                for half in range(2):
                    load_x(i, half).wait()

        with scope("norm"):
            @pl.when(ahead)
            def _():
                norm(i)

        with scope("stat"):
            @pl.when(busy)
            def _():
                wait(swap32(st, s % 2, sem_st))

        with scope("dz"):
            @pl.when(busy)
            def _():
                lse = merge(st, s % 2, 32)
                tacc[0:1, :] += weights(s) * lse
                grad_logits(s, lse)

        with scope("tabwait"):
            @pl.when(i == 0)
            def _():
                for j in range(len(blocks)):
                    tab_block(j).wait()

        with scope("logits"):
            @pl.when(ahead)
            def _():
                top = logits(i)
                st[i % 2, 0] = local_lse(i, top)

        with scope("meet"):
            @pl.when(i == 0)
            def _():
                pl.semaphore_wait(barrier, 31)

        with scope("hear"):
            @pl.when(ahead)
            def _():
                start(swap32(st, i % 2, sem_st))

            @pl.when(i >= 2)
            def _():
                hear_neighbours()

        with scope("partner"):
            @pl.when(in_range(s - 1))
            def _():
                add_partner(s - 1)

        with scope("serve_a"):
            serve_two(s, "x", 0, COL_A, r1a, zra, zla, fsa, fka, r3a, sem_a)

        with scope("serve_b"):
            serve_two(s, "y", COL_A, COL_B, r1b, zrb, zlb, fsb, fkb, r3b, sem_b)

        with scope("serve_c"):
            serve_c(s)

        with scope("tell"):
            @pl.when((i >= 1) & (i < last))
            def _():
                tell_neighbours()

        with scope("finish"):
            k = s - 5

            @pl.when(in_range(k))
            def _():
                load_own(k).start()

            @pl.when(in_range(k - 1))
            def _():
                finish(k - 1)

        with scope("de_last"):
            @pl.when(s == n_chunks)
            def _():
                embed_grad(s - 1)
                acc[...] = acc[...] * (1.0 / LOGIT_SCALE)
                pltpu.make_async_copy(acc, de_out, sem_out.at[2]).start()

        with scope("zero"):
            @pl.when(i == 0)
            def _():
                acc[...] = jnp.zeros_like(acc)

        with scope("de"):
            @pl.when(busy & (s < n_chunks - 1))
            def _():
                embed_grad(s)

            @pl.when(i + 1 < n_chunks)
            def _():
                for half in range(2):
                    load_x(i + 1, half).start()

        with scope("dh"):
            @pl.when(busy)
            def _():
                hidden_grad(s)

        return 0

    lax.fori_loop(0, last + 1, iteration, 0)
    with jax.named_scope("gain"):
        dg1[0, 0, :, 0:width] = jnp.sum(dgacc[...], axis=0, keepdims=True)
        dg1[0, 0, :, width : width + ROWS] = tacc[1:2, :]
        start(swap8(dg1, 0, sem_g1))
        wait(swap8(dg1, 0, sem_g1))
        dg2[0, 0] = sum(dg1[0, q] for q in range(8))
        start(swap4(dg2, 0, sem_g2))
        wait(swap4(dg2, 0, sem_g2))
        total = sum(dg2[0, q] for q in range(4))
        dg_out[...] = total[:, 0:width]
        loss_out[...] = tacc[0:1, :] - total[:, width : width + ROWS]
        for n in (n_chunks - 2, n_chunks - 1):
            store_dx(n).wait()
        pltpu.make_async_copy(acc, de_out, sem_out.at[2]).wait()


def hand_over_kernel(de_in, dx_in, dg_in, loss_in, de_out, dx_out, dg_out, loss_out, buf, sem):
    step = buf.shape[1]
    gets, puts = [], []
    for src, dst in ((de_in, de_out), (dx_in, dx_out)):
        rows = src.shape[0]
        for r in range(0, rows, step):
            n, some = len(gets), pl.ds(r, min(step, rows - r))
            here = buf.at[n, pl.ds(0, some.size)]
            gets.append(pltpu.make_async_copy(src.at[some], here, sem.at[0, n]))
            puts.append(pltpu.make_async_copy(here, dst.at[some], sem.at[1, n]))
    for get in gets:
        get.start()
    dg_out[...] = dg_in[...]
    loss_out[...] = jnp.sum(loss_in[...], keepdims=True)
    for get, put in zip(gets, puts):
        get.wait()
    for put in puts:
        put.start()
    for put in puts:
        put.wait()


def solution(mesh):
    def local_step(residual, labels, loss_mask, norm_gain, table_shard):
        tokens, width = residual.shape
        vocab = table_shard.shape[0]
        n_chunks = tokens // ROWS
        f32, bf16 = jnp.float32, jnp.bfloat16

        tok = jnp.stack([labels.astype(f32), loss_mask]).reshape(2, 16, 2, n_chunks, GROUP)
        tok = tok.transpose(0, 3, 2, 1, 4).reshape(2, n_chunks, ROWS)
        dma = pltpu.SemaphoreType.DMA
        vm = pltpu.VMEM
        slab = (GROUP, width)
        pair, ways = (2, 2), (2, 2, 3, 2)
        scratch = [vm((vocab, width), bf16), vm((2, 32, *slab), bf16), vm((vocab, ROWS), f32)]
        scratch += [vm((vocab, ROWS), bf16), vm((ROWS, vocab), bf16), vm((vocab, width), f32)]
        scratch += [vm((3, *GRID, *slab), f32), vm((*GRID, *slab), f32)]
        scratch += [vm((5, 4, 2, GROUP, n), f32) for n in (COL_A, COL_B)]
        scratch += [vm((3, 4, 2, GROUP, COL_C), f32), vm((5, 4, GROUP, COL_C), f32)]
        for n in (COL_A, COL_B):
            scratch += [vm((3, 3, 2, GROUP, n), f32)] * 2
        scratch += [vm((3, 3, GROUP, COL_C), f32)] * 2
        for n in (COL_A, COL_B):
            scratch += [vm((GROUP, n), f32), vm((GROUP, n), f32), vm((2, GROUP, n), f32)]
        scratch += [vm((2, 32, 1, ROWS), f32), vm((GROUP, ROWS), f32), vm((32, GROUP, 128), f32)]
        scratch += [vm(slab, f32), vm((2, *slab), bf16), vm((2, *slab), f32), vm(slab, f32)]
        scratch += [vm((1, n, 1, width + ROWS), f32) for n in (8, 4)]
        scratch += [dma((4,)), dma((8,)), dma((3,)), dma(pair), pltpu.SemaphoreType.REGULAR, pltpu.SemaphoreType.REGULAR((4,))]
        scratch += [dma((2, 2, 32)), dma((2, 1, 8)), dma((2, 1, 4))]
        scratch += [{"first": dma(pair), "z": dma(ways), "last": dma(pair)}] * 3
        whole = pl.BlockSpec(memory_space=pltpu.VMEM)
        raw = pl.BlockSpec(memory_space=pl.ANY)
        dx, de, dg, loss = pl.pallas_call(
            functools.partial(step_kernel, n_chunks),
            out_shape=(
                jax.ShapeDtypeStruct((n_chunks, GROUP, width), f32),
                jax.ShapeDtypeStruct((vocab, width), f32),
                jax.ShapeDtypeStruct((1, width), f32),
                jax.ShapeDtypeStruct((1, ROWS), f32),
            ),
            in_specs=[raw, whole, whole, raw],
            out_specs=(raw, raw, whole, whole),
            scratch_shapes=scratch,
            compiler_params=pltpu.CompilerParams(vmem_limit_bytes=VMEM_LIMIT, has_side_effects=True, collective_id=0),
            name="head_step",
        )(
            residual.reshape(16, 2, n_chunks, GROUP, width),
            tok,
            norm_gain.reshape(1, width),
            table_shard,
        )
        de, dx, dg, loss = pl.pallas_call(
            hand_over_kernel,
            out_shape=(
                jax.ShapeDtypeStruct((vocab, width), f32),
                jax.ShapeDtypeStruct((n_chunks * GROUP, width), f32),
                jax.ShapeDtypeStruct((1, width), f32),
                jax.ShapeDtypeStruct((1, 1), f32),
            ),
            in_specs=[raw, raw, whole, whole],
            out_specs=(raw, raw, whole, whole),
            scratch_shapes=[vm((16, 128, width), f32), dma((2, 16))],
            compiler_params=pltpu.CompilerParams(vmem_limit_bytes=VMEM_LIMIT),
            name="hand_over",
        )(de, dx.reshape(n_chunks * GROUP, width), dg, loss)
        return loss.reshape(()), dx, de, dg.reshape(width)

    return jax.shard_map(local_step, mesh=mesh, in_specs=(P(), P(), P(), P(), P("vp", None)), out_specs=(P(), P("vp", None), P("vp", None), P()), check_vma=False)
```

time: 611 us -> 583 us (0.954)
  other arithmetic: 23 us -> 0.79 us
    pallas_call x1, Pallas kernels: 581 us -> 558 us  [local_step(): pl.pallas_call(functools.partial(step_kernel, n_chunks), out_shape=(jax.S...]
    pallas_call x0 -> x1, Pallas kernels: none -> 20.8 us  [local_step(): pl.pallas_call(hand_over_kernel, out_shape=(jax.ShapeDtypeStruct((vocab,...]
    div x2 -> x0, other arithmetic: 20.4 us -> none  [the longest x1 19 us: local_step(): de / LOGIT_SCALE]
where the time goes in v2:
time: 583 us
  Pallas kernels  579 us (99%)
    pallas_call x1, Pallas kernels, local_step(): pl.pallas_call(functools.partial(step_kernel, n_chunks), out_shape=(jax.S...  558 us
    pallas_call x1, Pallas kernels, local_step(): pl.pallas_call(hand_over_kernel, out_shape=(jax.ShapeDtypeStruct((vocab,...  20.8 us

profile of v2, /device:TPU:0, one launch (start us, length us, event | category | flops | bytes accessed | tf_op | source)
XLA Modules:
  0.0 583.0 jit_solution(18282215182844524709)
XLA Ops:
  0.6 0.8 convert_element_type.3
  1.4 0.3 stack.9
  1.7 0.2 copy.11
  1.9 1.1 stack.10
  2.9 0.2 copy.12
  3.2 0.7 copy.14.tok
  3.9 558.3 %head_step.1 = (f32[32,8,4096]{2,1,0:T(8,128)}, f32[1544,4096]{1,0:T(8,128)}, f32[1,4096]{1,0:T(1,128)}, f32[1,256]{1,0:T(1,128)}) custom-call(bf16[16,2,32,8,4096]{4,3,2,1,0:T(8,128)(2,1)} %bitcast.res, f32[2,32,256]{2,1,0:T(8,128)} %copy.14.tok, f32[1,4096]{1,0:T(1,128)} %bitcast.10, bf16[1544,4096]{1,0:T(8,128)(2,1)} %tab.1), custom_call_target="tpu_custom_call" | custom-call | tf_op jit(solution)/shard_map/head_step/pallas_call | solution.py:614
  562.2 20.8 %hand_over.1 = (f32[1544,4096]{1,0:T(8,128)}, f32[256,4096]{1,0:T(8,128)}, f32[1,4096]{1,0:T(1,128)}, f32[1,1]{1,0:T(1,128)}) custom-call(f32[1544,4096]{1,0:T(8,128)} %get-tuple-element.12.de_in, f32[256,4096]{1,0:T(8,128)} %bitcast.8, f32[1,4096]{1,0:T(1,128)} %get-tuple-element.14.dg_in, f32[1,256]{1,0:T(1,128)} %get-tuple-element.15.loss_in), custom_call_target="tpu_custom_call" | custom-call | tf_op jit(solution)/shard_map/hand_over/pallas_call | solution.py:633
  (2 shorter events, 0.0 us)

commit v3 on v2

--- a/solution.py
+++ b/solution.py
@@ -15,14 +15,14 @@
 GROUP = 8
 ROWS = 32 * GROUP
 COL_A, COL_B, COL_C = 896, 1792, 1408
-DEPTH = 6
+DEPTH = 3
 VMEM_LIMIT = 67043328
 GRID = (4, 2, 2)
 
 
 def step_kernel(
     n_chunks, res, tok, gain, tab,
-    dx_out, de_out, dg_out, loss_out,
+    dx_out, de_out, sums_out,
     ev, h, zt, dzt, dz, acc, op, r0,
     r1a, r1b, r1c, r2c, zra, zla, zrb, zlb, zrc, zlc,
     fsa, fka, r3a, fsb, fkb, r3b,
@@ -50,7 +50,7 @@
     partner = dev(z, y, x, 1 - c)
 
     def load_x(n, half):
-        return pltpu.make_async_copy(res.at[:, half, n], h.at[n % 2, pl.ds(16 * half, 16)], sem_in.at[half])
+        return pltpu.make_async_copy(res.at[:, half, n], h.at[n % 3, pl.ds(16 * half, 16)], sem_in.at[half])
 
     def tab_block(j):
         a, m = blocks[j]
@@ -69,7 +69,7 @@
         return tok[1, pl.ds(n, 1), :] / tacc[2:3, :]
 
     def norm(n):
-        slot = n % 2
+        slot = n % 3
         pieces = range(0, width, 256)
 
         def piece(i, j):
@@ -92,14 +92,14 @@
                 h[slot, i, :, j : j + 256] = ((piece(i, j) * inv) * gain[:, j : j + 256]).astype(jnp.bfloat16)
             return 0
 
-        lax.fori_loop(0, 32, squares, 0, unroll=4)
+        lax.fori_loop(0, 32, squares, 0, unroll=8)
         mean = jnp.sum(ssq[...], axis=-1, keepdims=True) * (1.0 / width)
         ssq[...] = jnp.broadcast_to(lax.rsqrt(mean + NORM_EPS), ssq.shape)
-        lax.fori_loop(0, 32, scale, 0, unroll=4)
+        lax.fori_loop(0, 32, scale, 0, unroll=8)
 
     def logits(n):
         top = jnp.full((1, ROWS), -jnp.inf, jnp.float32)
-        hn = h[n % 2].reshape(ROWS, width)
+        hn = h[n % 3].reshape(ROWS, width)
         for a, m in blocks:
             t = lax.dot_general(ev[a : a + m, :], hn, (((1,), (1,)), ((), ())), preferred_element_type=jnp.float32)
             t = t * (1.0 / LOGIT_SCALE)
@@ -143,31 +143,32 @@
             dzt[a : a + m, :] = d
             dz[:, a : a + m] = d.T
 
-    def embed_grad(k):
+    def embed_grad(k, half):
         tile = width // 4
         for a, m in blocks:
-            for j in range(4):
+            for j in (2 * half, 2 * half + 1):
                 cols = pl.ds(j * tile, tile)
-                acc[a : a + m, cols] += jnp.dot(dzt[a : a + m, :], h[k % 2, :, :, cols].reshape(ROWS, tile), preferred_element_type=jnp.float32)
-
-    def send_p(half):
-        cols = pl.ds(half * (width // 2), width // 2)
-        return send(op.at[2, :, :, :, :, cols], r0.at[:, :, :, :, cols], sem_p.at[0, half], sem_p.at[1, half], partner)
-
-    def hidden_grad(k):
+                acc[a : a + m, cols] += jnp.dot(dzt[a : a + m, :], h[k % 3, :, :, cols].reshape(ROWS, tile), preferred_element_type=jnp.float32)
+
+    split = width * 3 // 4
+    parts = (pl.ds(0, split), pl.ds(split, width - split))
+
+    def send_p(part):
+        cols = parts[part]
+        return send(op.at[2, :, :, :, :, cols], r0.at[:, :, :, :, cols], sem_p.at[0, part], sem_p.at[1, part], partner)
+
+    def hidden_grad(k, part):
         own = k % 2
-        eq0 = 1 - c
-        where = (eq0 * own + (1 - eq0) * 2, c * own + (1 - c) * 2)
-        for half in range(2):
-            cols = pl.ds(half * (width // 2), width // 2)
-            r = jnp.dot(dz[...], ev[:, cols], preferred_element_type=jnp.float32)
-            for q in range(2):
-                op[where[q], :, :, :, :, cols] = r[q * 128 : (q + 1) * 128].reshape(4, 2, 2, 8, width // 2)
-            if half == 0:
-                @pl.when(k >= 1)
-                def _():
-                    pl.semaphore_wait(cred, 1)
-            send_p(half).start()
+        where = ((1 - c) * own + c * 2, c * own + (1 - c) * 2)
+        cols = parts[part]
+        r = jnp.dot(dz[...], ev[:, cols], preferred_element_type=jnp.float32)
+        for q in range(2):
+            op[where[q], :, :, :, :, cols] = r[q * 128 : (q + 1) * 128].reshape(4, 2, 2, 8, cols.size)
+        if part == 0:
+            @pl.when(k >= 1)
+            def _():
+                pl.semaphore_wait(cred, 1)
+        send_p(part).start()
 
     def add_partner(k):
         for half in range(2):
@@ -248,131 +249,130 @@
     def in_range(k):
         return (k >= 0) & (k < n_chunks)
 
-    def serve_two(s, axis, col, size, r1, zr, zl, fs, fk, r3, sem):
+    def two_axes(axis, col, size, r1, zr, zl, fs, fk, r3, sem):
         cols = pl.ds(col, size)
         first_nbr, last_nbr = (nbr_x, nbr_y) if axis == "x" else (nbr_y, nbr_x)
         q = y if axis == "x" else x
 
-        def copy1(k):
+        def first(k):
             src = op.at[k % 2, :, :, 1 - x, :, cols] if axis == "x" else op.at[k % 2, :, 1 - y, :, :, cols]
-            return hop(src, r1.at[k % 5], sem["first"], k, first_nbr)
-
-        def copy3(k):
+            return hop(src, r1.at[k % 3], sem["first"], k, first_nbr)
+
+        def last_hop(k):
             return hop(fs, r3.at[k % 2], sem["last"], k, last_nbr)
 
         def zc(k, t):
-            return z_copies(zr, zl, r1, k % 5, t, k % 3, sem["z"], k % 2)
-
-        k = s - 6
-
-        @pl.when(in_range(k))
-        def _():
-            copy3(k).wait()
-            dhf[:, cols] = fk[...] + r3[k % 2]
-
-        k5 = s - 5
-
-        @pl.when(in_range(k5))
-        def _():
-            z_wait(zc(k5, 2), 2)
-            sl = k5 % 5
-            fs[...] = r1[sl, z, 1 - q]
-            fk[...] = r1[sl, z, q]
-
-            @pl.when(z >= 1)
-            def _():
-                fs[...] += zr[2, k5 % 3, 1 - q]
-                fk[...] += zr[2, k5 % 3, q]
-
-            @pl.when(z <= 2)
-            def _():
-                fs[...] += zl[2, k5 % 3, 1 - q]
-                fk[...] += zl[2, k5 % 3, q]
-
-            copy3(k5).start()
-
-        for t, back in ((2, 4), (1, 3)):
-            kt = s - back
-
-            @pl.when(in_range(kt))
-            def _(kt=kt, t=t):
-                z_wait(zc(kt, t - 1), t - 1)
-                z_start(zc(kt, t), zr, zl, r1, kt % 5, t, kt % 3)
-
-        k2 = s - 2
-
-        @pl.when(in_range(k2))
-        def _():
-            copy1(k2).wait()
-            for b in range(4):
-                kept = op[k2 % 2, b, :, x, :, cols] if axis == "x" else op[k2 % 2, b, y, :, :, cols]
-                r1[k2 % 5, b] += kept
-            z_start(zc(k2, 0), zr, zl, r1, k2 % 5, 0, k2 % 3)
-
-        k1 = s - 1
-
-        @pl.when(in_range(k1))
-        def _():
-            copy1(k1).start()
-
-    def serve_c(s):
+            return z_copies(zr, zl, r1, k % 3, t, k % 2, sem["z"], k % 2)
+
+        def open_up(s):
+            @pl.when(in_range(s))
+            def _():
+                first(s).start()
+
+        def turn(s):
+            k = s - 3
+
+            @pl.when(in_range(k))
+            def _():
+                last_hop(k).wait()
+                dhf[:, cols] = fk[...] + r3[k % 2]
+
+            k2 = s - 2
+
+            @pl.when(in_range(k2))
+            def _():
+                z_wait(zc(k2, 2), 2)
+                sl, zs = k2 % 3, k2 % 2
+                fs[...] = r1[sl, z, 1 - q]
+                fk[...] = r1[sl, z, q]
+                for cond, buf in ((z >= 1, zr), (z <= 2, zl)):
+                    @pl.when(cond)
+                    def _(buf=buf):
+                        fs[...] += buf[2, zs, 1 - q]
+                        fk[...] += buf[2, zs, q]
+
+                last_hop(k2).start()
+
+            k1 = s - 1
+
+            @pl.when(in_range(k1))
+            def _():
+                first(k1).wait()
+                for b in range(4):
+                    kept = op[k1 % 2, b, :, x, :, cols] if axis == "x" else op[k1 % 2, b, y, :, :, cols]
+                    r1[k1 % 3, b] += kept
+                z_start(zc(k1, 0), zr, zl, r1, k1 % 3, 0, k1 % 2)
+
+        def move(s, t):
+            k = s - 2
+
+            @pl.when(in_range(k))
+            def _():
+                z_wait(zc(k, t - 1), t - 1)
+                z_start(zc(k, t), zr, zl, r1, k % 3, t, k % 2)
+
+        return open_up, turn, move
+
+    def three_axes():
         cols = pl.ds(COL_A + COL_B, COL_C)
 
-        def copy1(k):
+        def first(k):
             return hop(op.at[k % 2, :, :, 1 - x, :, cols], r1c.at[k % 3], sem_c["first"], k, nbr_x)
 
-        def copy2(k):
-            return hop(r1c.at[k % 3, :, 1 - y], r2c.at[k % 5], sem_c["last"], k, nbr_y)
+        def second(k):
+            return hop(r1c.at[k % 3, :, 1 - y], r2c.at[k % 3], sem_c["last"], k, nbr_y)
 
         def zc(k, t):
-            return z_copies(zrc, zlc, r2c, k % 5, t, k % 3, sem_c["z"], k % 2)
-
-        k = s - 6
-
-        @pl.when(in_range(k))
-        def _():
-            z_wait(zc(k, 2), 2)
-            dhf[:, cols] = r2c[k % 5, z]
-
-            @pl.when(z >= 1)
-            def _():
-                dhf[:, cols] += zrc[2, k % 3]
-
-            @pl.when(z <= 2)
-            def _():
-                dhf[:, cols] += zlc[2, k % 3]
-
-        for t, back in ((2, 5), (1, 4)):
-            kt = s - back
-
-            @pl.when(in_range(kt))
-            def _(kt=kt, t=t):
-                z_wait(zc(kt, t - 1), t - 1)
-                z_start(zc(kt, t), zrc, zlc, r2c, kt % 5, t, kt % 3)
-
-        k3 = s - 3
-
-        @pl.when(in_range(k3))
-        def _():
-            copy2(k3).wait()
-            for b in range(4):
-                r2c[k3 % 5, b] += r1c[k3 % 3, b, y]
-            z_start(zc(k3, 0), zrc, zlc, r2c, k3 % 5, 0, k3 % 3)
-
-        k2 = s - 2
-
-        @pl.when(in_range(k2))
-        def _():
-            copy1(k2).wait()
-            for b in range(4):
-                r1c[k2 % 3, b] += op[k2 % 2, b, :, x, :, cols]
-            copy2(k2).start()
-
-        k1 = s - 1
-
-        @pl.when(in_range(k1))
-        def _():
-            copy1(k1).start()
+            return z_copies(zrc, zlc, r2c, k % 3, t, k % 2, sem_c["z"], k % 2)
+
+        def open_up(s):
+            @pl.when(in_range(s))
+            def _():
+                first(s).start()
+
+        def turn(s):
+            k = s - 3
+
+            @pl.when(in_range(k))
+            def _():
+                z_wait(zc(k, 2), 2)
+                dhf[:, cols] = r2c[k % 3, z]
+                for cond, buf in ((z >= 1, zrc), (z <= 2, zlc)):
+                    @pl.when(cond)
+                    def _(buf=buf):
+                        dhf[:, cols] += buf[2, k % 2]
+
+            k2 = s - 2
+
+            @pl.when(in_range(k2))
+            def _():
+                second(k2).wait()
+                for b in range(4):
+                    r2c[k2 % 3, b] += r1c[k2 % 3, b, y]
+                z_start(zc(k2, 0), zrc, zlc, r2c, k2 % 3, 0, k2 % 2)
+
+            k1 = s - 1
+
+            @pl.when(in_range(k1))
+            def _():
+                first(k1).wait()
+                for b in range(4):
+                    r1c[k1 % 3, b] += op[k1 % 2, b, :, x, :, cols]
+                second(k1).start()
+
+        def move(s, t):
+            k = s - 3
+
+            @pl.when(in_range(k))
+            def _():
+                z_wait(zc(k, t - 1), t - 1)
+                z_start(zc(k, t), zrc, zlc, r2c, k % 3, t, k % 2)
+
+        return open_up, turn, move
+
+    open_a, turn_a, move_a = two_axes("x", 0, COL_A, r1a, zra, zla, fsa, fka, r3a, sem_a)
+    open_b, turn_b, move_b = two_axes("y", COL_A, COL_B, r1b, zrb, zlb, fsb, fkb, r3b, sem_b)
+    open_c, turn_c, move_c = three_axes()
 
     def finish(k):
         load_own(k).wait()
@@ -425,6 +425,15 @@
         tacc[...] = jnp.zeros_like(tacc)
         tacc[2:3, :] = jnp.broadcast_to(jnp.sum(tok[1], keepdims=True), (1, ROWS))
         dgacc[...] = jnp.zeros_like(dgacc)
+    with jax.named_scope("norm0"):
+        for half in range(2):
+            load_x(0, half).wait()
+        norm(0)
+        for half in range(2):
+            load_x(1, half).start()
+        for j in range(len(blocks)):
+            tab_block(j).wait()
+
     last = n_chunks + DEPTH
 
     def iteration(i, _):
@@ -433,111 +442,121 @@
         ahead = i < n_chunks
         scope = jax.named_scope
 
-        with scope("xwait"):
-            @pl.when(ahead)
-            def _():
-                for half in range(2):
-                    load_x(i, half).wait()
-
-        with scope("norm"):
-            @pl.when(ahead)
-            def _():
-                norm(i)
-
-        with scope("stat"):
-            @pl.when(busy)
-            def _():
-                wait(swap32(st, s % 2, sem_st))
-
-        with scope("dz"):
-            @pl.when(busy)
-            def _():
-                lse = merge(st, s % 2, 32)
-                tacc[0:1, :] += weights(s) * lse
-                grad_logits(s, lse)
-
-        with scope("tabwait"):
-            @pl.when(i == 0)
-            def _():
-                for j in range(len(blocks)):
-                    tab_block(j).wait()
-
         with scope("logits"):
             @pl.when(ahead)
             def _():
                 top = logits(i)
                 st[i % 2, 0] = local_lse(i, top)
 
-        with scope("meet"):
+        with scope("tell"):
             @pl.when(i == 0)
             def _():
                 pl.semaphore_wait(barrier, 31)
 
-        with scope("hear"):
             @pl.when(ahead)
             def _():
                 start(swap32(st, i % 2, sem_st))
 
-            @pl.when(i >= 2)
-            def _():
-                hear_neighbours()
+        with scope("b0"):
+            turn_b(s)
 
         with scope("partner"):
-            @pl.when(in_range(s - 1))
-            def _():
-                add_partner(s - 1)
-
-        with scope("serve_a"):
-            serve_two(s, "x", 0, COL_A, r1a, zra, zla, fsa, fka, r3a, sem_a)
-
-        with scope("serve_b"):
-            serve_two(s, "y", COL_A, COL_B, r1b, zrb, zlb, fsb, fkb, r3b, sem_b)
-
-        with scope("serve_c"):
-            serve_c(s)
-
-        with scope("tell"):
-            @pl.when((i >= 1) & (i < last))
-            def _():
-                tell_neighbours()
-
-        with scope("finish"):
-            k = s - 5
-
-            @pl.when(in_range(k))
-            def _():
-                load_own(k).start()
-
-            @pl.when(in_range(k - 1))
-            def _():
-                finish(k - 1)
-
-        with scope("de_last"):
-            @pl.when(s == n_chunks)
-            def _():
-                embed_grad(s - 1)
-                acc[...] = acc[...] * (1.0 / LOGIT_SCALE)
-                pltpu.make_async_copy(acc, de_out, sem_out.at[2]).start()
+            @pl.when(busy)
+            def _():
+                add_partner(s)
+
+            open_a(s)
+            open_b(s)
+            open_c(s)
+
+            @pl.when(in_range(s - 3))
+            def _():
+                load_own(s - 3).start()
 
         with scope("zero"):
             @pl.when(i == 0)
             def _():
                 acc[...] = jnp.zeros_like(acc)
 
-        with scope("de"):
-            @pl.when(busy & (s < n_chunks - 1))
-            def _():
-                embed_grad(s)
-
+        with scope("de0"):
+            @pl.when(busy)
+            def _():
+                embed_grad(s, 0)
+
+        with scope("ac0"):
+            turn_a(s)
+            turn_c(s)
+
+            @pl.when((i >= 1) & (i < last))
+            def _():
+                tell_neighbours()
+
+        with scope("finish"):
+            @pl.when(in_range(s - 3))
+            def _():
+                finish(s - 3)
+
+        with scope("de1"):
+            @pl.when(busy)
+            def _():
+                embed_grad(s, 1)
+
+            @pl.when(i == n_chunks)
+            def _():
+                pltpu.make_async_copy(acc, de_out, sem_out.at[2]).start()
+
+        with scope("hear"):
+            @pl.when((i >= 1) & (i < last))
+            def _():
+                hear_neighbours()
+
+        with scope("b1"):
+            move_b(i, 1)
+
+        with scope("norm"):
             @pl.when(i + 1 < n_chunks)
             def _():
                 for half in range(2):
-                    load_x(i + 1, half).start()
-
-        with scope("dh"):
-            @pl.when(busy)
-            def _():
-                hidden_grad(s)
+                    load_x(i + 1, half).wait()
+                norm(i + 1)
+
+            @pl.when(i + 2 < n_chunks)
+            def _():
+                for half in range(2):
+                    load_x(i + 2, half).start()
+
+        with scope("stat"):
+            @pl.when(ahead)
+            def _():
+                wait(swap32(st, i % 2, sem_st))
+
+        with scope("dz"):
+            @pl.when(ahead)
+            def _():
+                lse = merge(st, i % 2, 32)
+                tacc[0:1, :] += weights(i) * lse
+                grad_logits(i, lse)
+
+        with scope("ac1"):
+            move_a(i, 1)
+            move_c(i, 1)
+
+        with scope("dh0"):
+            @pl.when(ahead)
+            def _():
+                hidden_grad(i, 0)
+
+        with scope("b2"):
+            move_b(i, 2)
+
+        with scope("dh1"):
+            @pl.when(ahead)
+            def _():
+                hidden_grad(i, 1)
+
+        with scope("ac2"):
+            move_a(i, 2)
+            move_c(i, 2)
 
         return 0
 
@@ -551,14 +570,14 @@
         start(swap4(dg2, 0, sem_g2))
         wait(swap4(dg2, 0, sem_g2))
         total = sum(dg2[0, q] for q in range(4))
-        dg_out[...] = total[:, 0:width]
-        loss_out[...] = tacc[0:1, :] - total[:, width : width + ROWS]
+        sums_out[:, 0:width] = total[:, 0:width]
+        sums_out[:, width : width + ROWS] = tacc[0:1, :] - total[:, width : width + ROWS]
         for n in (n_chunks - 2, n_chunks - 1):
             store_dx(n).wait()
         pltpu.make_async_copy(acc, de_out, sem_out.at[2]).wait()
 
 
-def hand_over_kernel(de_in, dx_in, dg_in, loss_in, de_out, dx_out, dg_out, loss_out, buf, sem):
+def hand_over_kernel(de_in, dx_in, sums_in, de_out, dx_out, dg_out, loss_out, buf, sem):
     step = buf.shape[1]
     gets, puts = [], []
     for src, dst in ((de_in, de_out), (dx_in, dx_out)):
@@ -570,11 +589,15 @@
             puts.append(pltpu.make_async_copy(here, dst.at[some], sem.at[1, n]))
     for get in gets:
         get.start()
-    dg_out[...] = dg_in[...]
-    loss_out[...] = jnp.sum(loss_in[...], keepdims=True)
-    for get, put in zip(gets, puts):
+    width = de_in.shape[1]
+    dg_out[...] = sums_in[:, 0:width]
+    loss_out[...] = jnp.sum(sums_in[:, width : width + ROWS], keepdims=True)
+    for get in gets:
         get.wait()
-    for put in puts:
+    scaled = de_in.shape[0]
+    for n, put in enumerate(puts):
+        if n * step < scaled:
+            buf[n] = buf[n] * (1.0 / LOGIT_SCALE)
         put.start()
     for put in puts:
         put.wait()
@@ -593,14 +616,14 @@
         vm = pltpu.VMEM
         slab = (GROUP, width)
         pair, ways = (2, 2), (2, 2, 3, 2)
-        scratch = [vm((vocab, width), bf16), vm((2, 32, *slab), bf16), vm((vocab, ROWS), f32)]
+        scratch = [vm((vocab, width), bf16), vm((3, 32, *slab), bf16), vm((vocab, ROWS), f32)]
         scratch += [vm((vocab, ROWS), bf16), vm((ROWS, vocab), bf16), vm((vocab, width), f32)]
         scratch += [vm((3, *GRID, *slab), f32), vm((*GRID, *slab), f32)]
-        scratch += [vm((5, 4, 2, GROUP, n), f32) for n in (COL_A, COL_B)]
-        scratch += [vm((3, 4, 2, GROUP, COL_C), f32), vm((5, 4, GROUP, COL_C), f32)]
+        scratch += [vm((3, 4, 2, GROUP, n), f32) for n in (COL_A, COL_B)]
+        scratch += [vm((3, 4, 2, GROUP, COL_C), f32), vm((3, 4, GROUP, COL_C), f32)]
         for n in (COL_A, COL_B):
-            scratch += [vm((3, 3, 2, GROUP, n), f32)] * 2
-        scratch += [vm((3, 3, GROUP, COL_C), f32)] * 2
+            scratch += [vm((3, 2, 2, GROUP, n), f32)] * 2
+        scratch += [vm((3, 2, GROUP, COL_C), f32)] * 2
         for n in (COL_A, COL_B):
             scratch += [vm((GROUP, n), f32), vm((GROUP, n), f32), vm((2, GROUP, n), f32)]
         scratch += [vm((2, 32, 1, ROWS), f32), vm((GROUP, ROWS), f32), vm((32, GROUP, 128), f32)]
@@ -611,16 +634,15 @@
         scratch += [{"first": dma(pair), "z": dma(ways), "last": dma(pair)}] * 3
         whole = pl.BlockSpec(memory_space=pltpu.VMEM)
         raw = pl.BlockSpec(memory_space=pl.ANY)
-        dx, de, dg, loss = pl.pallas_call(
+        dx, de, sums = pl.pallas_call(
             functools.partial(step_kernel, n_chunks),
             out_shape=(
                 jax.ShapeDtypeStruct((n_chunks, GROUP, width), f32),
                 jax.ShapeDtypeStruct((vocab, width), f32),
-                jax.ShapeDtypeStruct((1, width), f32),
-                jax.ShapeDtypeStruct((1, ROWS), f32),
+                jax.ShapeDtypeStruct((1, width + ROWS), f32),
             ),
             in_specs=[raw, whole, whole, raw],
-            out_specs=(raw, raw, whole, whole),
+            out_specs=(raw, raw, whole),
             scratch_shapes=scratch,
             compiler_params=pltpu.CompilerParams(vmem_limit_bytes=VMEM_LIMIT, has_side_effects=True, collective_id=0),
             name="head_step",
@@ -638,12 +660,12 @@
                 jax.ShapeDtypeStruct((1, width), f32),
                 jax.ShapeDtypeStruct((1, 1), f32),
             ),
-            in_specs=[raw, raw, whole, whole],
+            in_specs=[raw, raw, whole],
             out_specs=(raw, raw, whole, whole),
             scratch_shapes=[vm((16, 128, width), f32), dma((2, 16))],
             compiler_params=pltpu.CompilerParams(vmem_limit_bytes=VMEM_LIMIT),
             name="hand_over",
-        )(de, dx.reshape(n_chunks * GROUP, width), dg, loss)
+        )(de, dx.reshape(n_chunks * GROUP, width), sums)
         return loss.reshape(()), dx, de, dg.reshape(width)
 
     return jax.shard_map(local_step, mesh=mesh, in_specs=(P(), P(), P(), P(), P("vp", None)), out_specs=(P(), P("vp", None), P("vp", None), P()), check_vma=False)

time: 583 us -> 569 us (0.976)
  Pallas kernels: 579 us -> 565 us
    pallas_call x1, Pallas kernels: 558 us -> 544 us  [local_step(): pl.pallas_call(functools.partial(step_kernel, n_chunks), out_shape=(jax.S...]
where the time goes in v3:
time: 569 us
  Pallas kernels  565 us (99%)
    pallas_call x1, Pallas kernels, local_step(): pl.pallas_call(functools.partial(step_kernel, n_chunks), out_shape=(jax.S...  544 us
    pallas_call x1, Pallas kernels, local_step(): pl.pallas_call(hand_over_kernel, out_shape=(jax.ShapeDtypeStruct((vocab,...  20.9 us

profile of v3, /device:TPU:0, one launch (start us, length us, event | category | flops | bytes accessed | tf_op | source)
XLA Modules:
  0.0 569.1 jit_solution(6894020386563158800)
XLA Ops:
  0.6 0.8 convert_element_type.3
  1.4 0.3 stack.9
  1.7 0.2 copy.11
  1.9 1.1 stack.10
  2.9 0.2 copy.12
  3.2 0.7 copy.14.tok
  3.9 544.1 %head_step.1 = (f32[32,8,4096]{2,1,0:T(8,128)}, f32[1544,4096]{1,0:T(8,128)}, f32[1,4352]{1,0:T(1,128)}) custom-call(bf16[16,2,32,8,4096]{4,3,2,1,0:T(8,128)(2,1)} %bitcast.res, f32[2,32,256]{2,1,0:T(8,128)} %copy.14.tok, f32[1,4096]{1,0:T(1,128)} %bitcast.10, bf16[1544,4096]{1,0:T(8,128)(2,1)} %tab.1), custom_call_target="tpu_custom_call" | custom-call | tf_op jit(solution)/shard_map/head_step/pallas_call | solution.py:637
  548.0 20.9 %hand_over.1 = (f32[1544,4096]{1,0:T(8,128)}, f32[256,4096]{1,0:T(8,128)}, f32[1,4096]{1,0:T(1,128)}, f32[1,1]{1,0:T(1,128)}) custom-call(f32[1544,4096]{1,0:T(8,128)} %get-tuple-element.11.de_in, f32[256,4096]{1,0:T(8,128)} %bitcast.8, f32[1,4352]{1,0:T(1,128)} %get-tuple-element.13.sums_in), custom_call_target="tpu_custom_call" | custom-call | tf_op jit(solution)/shard_map/hand_over/pallas_call | solution.py:655
  (2 shorter events, 0.0 us)

commit v4 on v3

--- a/solution.py
+++ b/solution.py
@@ -10,6 +10,7 @@
 VOCAB_REAL = 49155
 LOGIT_SCALE = 6.0
 NORM_EPS = 1e-6
+INV_SCALE = 1.0 / LOGIT_SCALE
 MESH = pl.DeviceIdType.MESH
 
 GROUP = 8
@@ -76,14 +77,14 @@
             return h[slot, i, :, j : j + 256].astype(jnp.float32)
 
         def squares(i, _):
-            parts = []
-            for j in pieces:
+            sums = [None] * 4
+            for n_piece, j in enumerate(pieces):
                 sq = piece(i, j)
                 sq = sq * sq
-                parts.append(sq[:, :128] + sq[:, 128:])
-            while len(parts) > 1:
-                parts = [p + q for p, q in zip(parts[::2], parts[1::2])]
-            ssq[i] = parts[0]
+                for b in range(2):
+                    part, to = sq[:, 128 * b : 128 * (b + 1)], 2 * (n_piece % 2) + b
+                    sums[to] = part if sums[to] is None else sums[to] + part
+            ssq[i] = (sums[0] + sums[1]) + (sums[2] + sums[3])
             return 0
 
         def scale(i, _):
@@ -92,17 +93,17 @@
                 h[slot, i, :, j : j + 256] = ((piece(i, j) * inv) * gain[:, j : j + 256]).astype(jnp.bfloat16)
             return 0
 
-        lax.fori_loop(0, 32, squares, 0, unroll=8)
+        lax.fori_loop(0, 32, squares, 0, unroll=4)
         mean = jnp.sum(ssq[...], axis=-1, keepdims=True) * (1.0 / width)
         ssq[...] = jnp.broadcast_to(lax.rsqrt(mean + NORM_EPS), ssq.shape)
-        lax.fori_loop(0, 32, scale, 0, unroll=8)
+        lax.fori_loop(0, 32, scale, 0, unroll=4)
 
     def logits(n):
         top = jnp.full((1, ROWS), -jnp.inf, jnp.float32)
         hn = h[n % 3].reshape(ROWS, width)
         for a, m in blocks:
             t = lax.dot_general(ev[a : a + m, :], hn, (((1,), (1,)), ((), ())), preferred_element_type=jnp.float32)
-            t = t * (1.0 / LOGIT_SCALE)
+            t = t * INV_SCALE
             ids = me * vocab + a + lax.broadcasted_iota(jnp.int32, (m, ROWS), 0)
             t = jnp.where(ids < VOCAB_REAL, t, -jnp.inf)
             zt[a : a + m, :] = t
@@ -123,7 +124,7 @@
             return s + jnp.sum(e, axis=0), t + jnp.sum(hit, axis=0)
 
         zero = jnp.zeros((8, ROWS), jnp.float32)
-        s, t = lax.fori_loop(0, full_tiles, lambda i, v: part(pl.multiple_of(i * 128, 128), 128, *v), (zero, zero))
+        s, t = lax.fori_loop(0, full_tiles, lambda i, v: part(pl.multiple_of(i * 128, 128), 128, *v), (zero, zero), unroll=4)
         s, t = part(full_tiles * 128, tail, s, t)
         tacc[1:2, :] += weights(n) * jnp.sum(t, axis=0, keepdims=True)
         return top + jnp.log(jnp.sum(s, axis=0, keepdims=True))
@@ -330,26 +331,38 @@
             def _():
                 first(s).start()
 
+        end = n_chunks - 1
+
+        def to_z(k):
+            second(k).wait()
+            for b in range(4):
+                r2c[k % 3, b] += r1c[k % 3, b, y]
+            z_start(zc(k, 0), zrc, zlc, r2c, k % 3, 0, k % 2)
+
+        def along_z(k, t):
+            z_wait(zc(k, t - 1), t - 1)
+            z_start(zc(k, t), zrc, zlc, r2c, k % 3, t, k % 2)
+
+        def off_z(k):
+            z_wait(zc(k, 2), 2)
+            dhf[:, cols] = r2c[k % 3, z]
+            for cond, buf in ((z >= 1, zrc), (z <= 2, zlc)):
+                @pl.when(cond)
+                def _(buf=buf):
+                    dhf[:, cols] += buf[2, k % 2]
+
         def turn(s):
-            k = s - 3
-
-            @pl.when(in_range(k))
-            def _():
-                z_wait(zc(k, 2), 2)
-                dhf[:, cols] = r2c[k % 3, z]
-                for cond, buf in ((z >= 1, zrc), (z <= 2, zlc)):
-                    @pl.when(cond)
-                    def _(buf=buf):
-                        dhf[:, cols] += buf[2, k % 2]
-
-            k2 = s - 2
-
-            @pl.when(in_range(k2))
-            def _():
-                second(k2).wait()
-                for b in range(4):
-                    r2c[k2 % 3, b] += r1c[k2 % 3, b, y]
-                z_start(zc(k2, 0), zrc, zlc, r2c, k2 % 3, 0, k2 % 2)
+            @pl.when(in_range(s - 3) & (s - 3 != end))
+            def _():
+                off_z(s - 3)
+
+            @pl.when(in_range(s - 2) & (s - 2 != end))
+            def _():
+                to_z(s - 2)
+
+            @pl.when(s - 2 == end)
+            def _():
+                along_z(end, 1)
 
             k1 = s - 1
 
@@ -361,12 +374,22 @@
                 second(k1).start()
 
         def move(s, t):
-            k = s - 3
-
-            @pl.when(in_range(k))
-            def _():
-                z_wait(zc(k, t - 1), t - 1)
-                z_start(zc(k, t), zrc, zlc, r2c, k % 3, t, k % 2)
+            @pl.when(in_range(s - 3) & (s - 3 != end))
+            def _():
+                along_z(s - 3, t)
+
+            if t == 1:
+                @pl.when(s - 3 == end)
+                def _():
+                    along_z(end, 2)
+            else:
+                @pl.when(s - 2 == end)
+                def _():
+                    to_z(end)
+
+                @pl.when(s - 3 == end)
+                def _():
+                    off_z(end)
 
         return open_up, turn, move
 
@@ -382,12 +405,13 @@
             store_dx(k - 2).wait()
 
         xo = xr[k % 2].astype(jnp.float32)
+        dh = dhf[...] * INV_SCALE
+        u = dh * gain[...]
         inv = lax.rsqrt(jnp.mean(xo * xo, axis=-1, keepdims=True) + NORM_EPS)
+        slope = inv * jnp.mean(u * xo, axis=-1, keepdims=True)
         xh = xo * inv
-        dh = dhf[...] / LOGIT_SCALE
         dgacc[...] += dh * xh
-        u = dh * gain[...]
-        dxb[k % 2] = inv * (u - xh * jnp.mean(u * xh, axis=-1, keepdims=True))
+        dxb[k % 2] = inv * (u - xh * slope)
         store_dx(k).start()
 
     def tell_neighbours():
@@ -469,10 +493,6 @@
             open_b(s)
             open_c(s)
 
-            @pl.when(in_range(s - 3))
-            def _():
-                load_own(s - 3).start()
-
         with scope("zero"):
             @pl.when(i == 0)
             def _():
@@ -495,6 +515,10 @@
             @pl.when(in_range(s - 3))
             def _():
                 finish(s - 3)
+
+            @pl.when(in_range(s - 2))
+            def _():
+                load_own(s - 2).start()
 
         with scope("de1"):
             @pl.when(busy)
@@ -597,7 +621,7 @@
     scaled = de_in.shape[0]
     for n, put in enumerate(puts):
         if n * step < scaled:
-            buf[n] = buf[n] * (1.0 / LOGIT_SCALE)
+            buf[n] = buf[n] * INV_SCALE
         put.start()
     for put in puts:
         put.wait()

time: 569 us -> 560 us (0.984)
  Pallas kernels: 565 us -> 556 us
    pallas_call x1, Pallas kernels: 544 us -> 535 us  [local_step(): pl.pallas_call(functools.partial(step_kernel, n_chunks), out_shape=(jax.S...]
where the time goes in v4:
time: 560 us
  Pallas kernels  556 us (99%)
    pallas_call x1, Pallas kernels, local_step(): pl.pallas_call(functools.partial(step_kernel, n_chunks), out_shape=(jax.S...  535 us
    pallas_call x1, Pallas kernels, local_step(): pl.pallas_call(hand_over_kernel, out_shape=(jax.ShapeDtypeStruct((vocab,...  20.9 us

profile of v4, /device:TPU:0, one launch (start us, length us, event | category | flops | bytes accessed | tf_op | source)
XLA Modules:
  0.0 559.7 jit_solution(4175764376595173746)
XLA Ops:
  0.6 0.8 convert_element_type.3
  1.4 0.3 stack.9
  1.7 0.2 copy.11
  1.9 1.1 stack.10
  2.9 0.2 copy.12
  3.2 0.7 copy.14.tok
  3.9 534.6 %head_step.1 = (f32[32,8,4096]{2,1,0:T(8,128)}, f32[1544,4096]{1,0:T(8,128)}, f32[1,4352]{1,0:T(1,128)}) custom-call(bf16[16,2,32,8,4096]{4,3,2,1,0:T(8,128)(2,1)} %bitcast.res, f32[2,32,256]{2,1,0:T(8,128)} %copy.14.tok, f32[1,4096]{1,0:T(1,128)} %bitcast.10, bf16[1544,4096]{1,0:T(8,128)(2,1)} %tab.1), custom_call_target="tpu_custom_call" | custom-call | tf_op jit(solution)/shard_map/head_step/pallas_call | solution.py:661
  538.6 20.9 %hand_over.1 = (f32[1544,4096]{1,0:T(8,128)}, f32[256,4096]{1,0:T(8,128)}, f32[1,4096]{1,0:T(1,128)}, f32[1,1]{1,0:T(1,128)}) custom-call(f32[1544,4096]{1,0:T(8,128)} %get-tuple-element.11.de_in, f32[256,4096]{1,0:T(8,128)} %bitcast.8, f32[1,4352]{1,0:T(1,128)} %get-tuple-element.13.sums_in), custom_call_target="tpu_custom_call" | custom-call | tf_op jit(solution)/shard_map/hand_over/pallas_call | solution.py:679
  (2 shorter events, 0.0 us)

commit v5 on v4

--- a/solution.py
+++ b/solution.py
@@ -40,11 +40,14 @@
     def dev(zz, yy, xx, cc):
         return (((zz * 2 + yy) * 2 + xx) * 2 + cc,)
 
+    def par(k):
+        return k % 2
+
     def send(src, dst, ssem, rsem, to):
         return pltpu.make_async_remote_copy(src, dst, ssem, rsem, device_id=to, device_id_type=MESH)
 
     def hop(src, dst, sem, k, to):
-        return send(src, dst, sem.at[0, k % 2], sem.at[1, k % 2], to)
+        return send(src, dst, sem.at[0, par(k)], sem.at[1, par(k)], to)
 
     nbr_x, nbr_y = dev(z, y, 1 - x, c), dev(z, 1 - y, x, c)
     nbr_r, nbr_l = dev(z + 1, y, x, c), dev(z - 1, y, x, c)
@@ -58,10 +61,10 @@
         return pltpu.make_async_copy(tab.at[pl.ds(a, m)], ev.at[pl.ds(a, m)], sem_tab.at[j])
 
     def load_own(n):
-        return pltpu.make_async_copy(res.at[me // 2, me % 2, n], xr.at[n % 2], sem_in.at[2 + n % 2])
+        return pltpu.make_async_copy(res.at[me // 2, me % 2, n], xr.at[par(n)], sem_in.at[2 + par(n)])
 
     def store_dx(n):
-        return pltpu.make_async_copy(dxb.at[n % 2], dx_out.at[n], sem_out.at[n % 2])
+        return pltpu.make_async_copy(dxb.at[par(n)], dx_out.at[n], sem_out.at[par(n)])
 
     def label_rows(n):
         return tok[0, pl.ds(n, 1), :].astype(jnp.int32) - me * vocab
@@ -159,7 +162,7 @@
         return send(op.at[2, :, :, :, :, cols], r0.at[:, :, :, :, cols], sem_p.at[0, part], sem_p.at[1, part], partner)
 
     def hidden_grad(k, part):
-        own = k % 2
+        own = par(k)
         where = ((1 - c) * own + c * 2, c * own + (1 - c) * 2)
         cols = parts[part]
         r = jnp.dot(dz[...], ev[:, cols], preferred_element_type=jnp.float32)
@@ -176,7 +179,7 @@
             send_p(half).wait()
 
         def body(i, _):
-            op[k % 2, i] += r0[i]
+            op[par(k), i] += r0[i]
             return 0
 
         lax.fori_loop(0, 4, body, 0)
@@ -256,14 +259,14 @@
         q = y if axis == "x" else x
 
         def first(k):
-            src = op.at[k % 2, :, :, 1 - x, :, cols] if axis == "x" else op.at[k % 2, :, 1 - y, :, :, cols]
+            src = op.at[par(k), :, :, 1 - x, :, cols] if axis == "x" else op.at[par(k), :, 1 - y, :, :, cols]
             return hop(src, r1.at[k % 3], sem["first"], k, first_nbr)
 
         def last_hop(k):
-            return hop(fs, r3.at[k % 2], sem["last"], k, last_nbr)
+            return hop(fs, r3.at[par(k)], sem["last"], k, last_nbr)
 
         def zc(k, t):
-            return z_copies(zr, zl, r1, k % 3, t, k % 2, sem["z"], k % 2)
+            return z_copies(zr, zl, r1, k % 3, t, par(k), sem["z"], par(k))
 
         def open_up(s):
             @pl.when(in_range(s))
@@ -276,14 +279,14 @@
             @pl.when(in_range(k))
             def _():
                 last_hop(k).wait()
-                dhf[:, cols] = fk[...] + r3[k % 2]
+                dhf[:, cols] = fk[...] + r3[par(k)]
 
             k2 = s - 2
 
             @pl.when(in_range(k2))
             def _():
                 z_wait(zc(k2, 2), 2)
-                sl, zs = k2 % 3, k2 % 2
+                sl, zs = k2 % 3, par(k2)
                 fs[...] = r1[sl, z, 1 - q]
                 fk[...] = r1[sl, z, q]
                 for cond, buf in ((z >= 1, zr), (z <= 2, zl)):
@@ -300,9 +303,9 @@
             def _():
                 first(k1).wait()
                 for b in range(4):
-                    kept = op[k1 % 2, b, :, x, :, cols] if axis == "x" else op[k1 % 2, b, y, :, :, cols]
+                    kept = op[par(k1), b, :, x, :, cols] if axis == "x" else op[par(k1), b, y, :, :, cols]
                     r1[k1 % 3, b] += kept
-                z_start(zc(k1, 0), zr, zl, r1, k1 % 3, 0, k1 % 2)
+                z_start(zc(k1, 0), zr, zl, r1, k1 % 3, 0, par(k1))
 
         def move(s, t):
             k = s - 2
@@ -310,7 +313,7 @@
             @pl.when(in_range(k))
             def _():
                 z_wait(zc(k, t - 1), t - 1)
-                z_start(zc(k, t), zr, zl, r1, k % 3, t, k % 2)
+                z_start(zc(k, t), zr, zl, r1, k % 3, t, par(k))
 
         return open_up, turn, move
 
@@ -318,13 +321,13 @@
         cols = pl.ds(COL_A + COL_B, COL_C)
 
         def first(k):
-            return hop(op.at[k % 2, :, :, 1 - x, :, cols], r1c.at[k % 3], sem_c["first"], k, nbr_x)
+            return hop(op.at[par(k), :, :, 1 - x, :, cols], r1c.at[k % 3], sem_c["first"], k, nbr_x)
 
         def second(k):
             return hop(r1c.at[k % 3, :, 1 - y], r2c.at[k % 3], sem_c["last"], k, nbr_y)
 
         def zc(k, t):
-            return z_copies(zrc, zlc, r2c, k % 3, t, k % 2, sem_c["z"], k % 2)
+            return z_copies(zrc, zlc, r2c, k % 3, t, par(k), sem_c["z"], par(k))
 
         def open_up(s):
             @pl.when(in_range(s))
@@ -337,11 +340,11 @@
             second(k).wait()
             for b in range(4):
                 r2c[k % 3, b] += r1c[k % 3, b, y]
-            z_start(zc(k, 0), zrc, zlc, r2c, k % 3, 0, k % 2)
+            z_start(zc(k, 0), zrc, zlc, r2c, k % 3, 0, par(k))
 
         def along_z(k, t):
             z_wait(zc(k, t - 1), t - 1)
-            z_start(zc(k, t), zrc, zlc, r2c, k % 3, t, k % 2)
+            z_start(zc(k, t), zrc, zlc, r2c, k % 3, t, par(k))
 
         def off_z(k):
             z_wait(zc(k, 2), 2)
@@ -349,7 +352,7 @@
             for cond, buf in ((z >= 1, zrc), (z <= 2, zlc)):
                 @pl.when(cond)
                 def _(buf=buf):
-                    dhf[:, cols] += buf[2, k % 2]
+                    dhf[:, cols] += buf[2, par(k)]
 
         def turn(s):
             @pl.when(in_range(s - 3) & (s - 3 != end))
@@ -370,7 +373,7 @@
             def _():
                 first(k1).wait()
                 for b in range(4):
-                    r1c[k1 % 3, b] += op[k1 % 2, b, :, x, :, cols]
+                    r1c[k1 % 3, b] += op[par(k1), b, :, x, :, cols]
                 second(k1).start()
 
         def move(s, t):
@@ -397,21 +400,23 @@
     open_b, turn_b, move_b = two_axes("y", COL_A, COL_B, r1b, zrb, zlb, fsb, fkb, r3b, sem_b)
     open_c, turn_c, move_c = three_axes()
 
-    def finish(k):
+    def finish(k, beside=()):
         load_own(k).wait()
 
         @pl.when(k >= 2)
         def _():
             store_dx(k - 2).wait()
 
-        xo = xr[k % 2].astype(jnp.float32)
+        xo = xr[par(k)].astype(jnp.float32)
         dh = dhf[...] * INV_SCALE
         u = dh * gain[...]
         inv = lax.rsqrt(jnp.mean(xo * xo, axis=-1, keepdims=True) + NORM_EPS)
         slope = inv * jnp.mean(u * xo, axis=-1, keepdims=True)
         xh = xo * inv
         dgacc[...] += dh * xh
-        dxb[k % 2] = inv * (u - xh * slope)
+        dxb[par(k)] = inv * (u - xh * slope)
+        for work in beside:
+            work()
         store_dx(k).start()
 
     def tell_neighbours():
@@ -470,7 +475,7 @@
             @pl.when(ahead)
             def _():
                 top = logits(i)
-                st[i % 2, 0] = local_lse(i, top)
+                st[par(i), 0] = local_lse(i, top)
 
         with scope("tell"):
             @pl.when(i == 0)
@@ -479,7 +484,7 @@
 
             @pl.when(ahead)
             def _():
-                start(swap32(st, i % 2, sem_st))
+                start(swap32(st, par(i), sem_st))
 
         with scope("b0"):
             turn_b(s)
@@ -507,12 +512,20 @@
             turn_a(s)
             turn_c(s)
 
-            @pl.when((i >= 1) & (i < last))
+            @pl.when((i >= 1) & (i < last - 1))
             def _():
                 tell_neighbours()
 
         with scope("finish"):
-            @pl.when(in_range(s - 3))
+            @pl.when(busy & (s >= 3))
+            def _():
+                finish(s - 3, (lambda: embed_grad(s, 1),))
+
+            @pl.when(busy & (s < 3))
+            def _():
+                embed_grad(s, 1)
+
+            @pl.when(s >= n_chunks)
             def _():
                 finish(s - 3)
 
@@ -521,16 +534,12 @@
                 load_own(s - 2).start()
 
         with scope("de1"):
-            @pl.when(busy)
-            def _():
-                embed_grad(s, 1)
-
             @pl.when(i == n_chunks)
             def _():
                 pltpu.make_async_copy(acc, de_out, sem_out.at[2]).start()
 
         with scope("hear"):
-            @pl.when((i >= 1) & (i < last))
+            @pl.when((i >= 1) & (i < last - 1))
             def _():
                 hear_neighbours()
 
@@ -552,12 +561,12 @@
         with scope("stat"):
             @pl.when(ahead)
             def _():
-                wait(swap32(st, i % 2, sem_st))
+                wait(swap32(st, par(i), sem_st))
 
         with scope("dz"):
             @pl.when(ahead)
             def _():
-                lse = merge(st, i % 2, 32)
+                lse = merge(st, par(i), 32)
                 tacc[0:1, :] += weights(i) * lse
                 grad_logits(i, lse)
 
@@ -601,7 +610,7 @@
         pltpu.make_async_copy(acc, de_out, sem_out.at[2]).wait()
 
 
-def hand_over_kernel(de_in, dx_in, sums_in, de_out, dx_out, dg_out, loss_out, buf, sem):
+def hand_over_kernel(de_in, dx_in, sums_in, de_out, dx_out, dg_out, loss_out, buf, row, sem, row_sem):
     step = buf.shape[1]
     gets, puts = [], []
     for src, dst in ((de_in, de_out), (dx_in, dx_out)):
@@ -614,8 +623,12 @@
     for get in gets:
         get.start()
     width = de_in.shape[1]
-    dg_out[...] = sums_in[:, 0:width]
-    loss_out[...] = jnp.sum(sums_in[:, width : width + ROWS], keepdims=True)
+    get_row = pltpu.make_async_copy(sums_in, row, row_sem.at[0])
+    put_row = pltpu.make_async_copy(row.at[:, pl.ds(0, width)], dg_out, row_sem.at[1])
+    get_row.start()
+    get_row.wait()
+    put_row.start()
+    loss_out[...] = jnp.sum(row[:, width : width + ROWS], keepdims=True)
     for get in gets:
         get.wait()
     scaled = de_in.shape[0]
@@ -623,7 +636,7 @@
         if n * step < scaled:
             buf[n] = buf[n] * INV_SCALE
         put.start()
-    for put in puts:
+    for put in (put_row, *puts):
         put.wait()
 
 
@@ -655,7 +668,7 @@
         scratch += [vm((1, n, 1, width + ROWS), f32) for n in (8, 4)]
         scratch += [dma((4,)), dma((8,)), dma((3,)), dma(pair), pltpu.SemaphoreType.REGULAR, pltpu.SemaphoreType.REGULAR((4,))]
         scratch += [dma((2, 2, 32)), dma((2, 1, 8)), dma((2, 1, 4))]
-        scratch += [{"first": dma(pair), "z": dma(ways), "last": dma(pair)}] * 3
+        scratch += [{"first": dma(pair), "z": dma(ways), "last": dma(pair)} for _ in "abc"]
         whole = pl.BlockSpec(memory_space=pltpu.VMEM)
         raw = pl.BlockSpec(memory_space=pl.ANY)
         dx, de, sums = pl.pallas_call(
@@ -684,9 +697,9 @@
                 jax.ShapeDtypeStruct((1, width), f32),
                 jax.ShapeDtypeStruct((1, 1), f32),
             ),
-            in_specs=[raw, raw, whole],
-            out_specs=(raw, raw, whole, whole),
-            scratch_shapes=[vm((16, 128, width), f32), dma((2, 16))],
+            in_specs=[raw] * 3,
+            out_specs=(raw, raw, raw, whole),
+            scratch_shapes=[vm((16, 128, width), f32), vm((1, width + ROWS), f32), dma((2, 16)), dma((2,))],
             compiler_params=pltpu.CompilerParams(vmem_limit_bytes=VMEM_LIMIT),
             name="hand_over",
         )(de, dx.reshape(n_chunks * GROUP, width), sums)

time: 560 us -> 558 us (level)
  no operation moved by 1% of the time
where the time goes in v5:
time: 558 us
  Pallas kernels  554 us (99%)
    pallas_call x1, Pallas kernels, local_step(): pl.pallas_call(functools.partial(step_kernel, n_chunks), out_shape=(jax.S...  534 us
    pallas_call x1, Pallas kernels, local_step(): pl.pallas_call(hand_over_kernel, out_shape=(jax.ShapeDtypeStruct((vocab,...  20.1 us

profile of v5, /device:TPU:0, one launch (start us, length us, event | category | flops | bytes accessed | tf_op | source)
XLA Modules:
  0.0 558.2 jit_solution(13820086551758796628)
XLA Ops:
  0.6 0.8 convert_element_type.3
  1.4 0.3 stack.9
  1.7 0.2 copy.11
  1.9 1.1 stack.10
  2.9 0.2 copy.12
  3.2 0.7 copy.14.tok
  3.9 533.9 %head_step.1 = (f32[32,8,4096]{2,1,0:T(8,128)}, f32[1544,4096]{1,0:T(8,128)}, f32[1,4352]{1,0:T(1,128)}) custom-call(bf16[16,2,32,8,4096]{4,3,2,1,0:T(8,128)(2,1)} %bitcast.res, f32[2,32,256]{2,1,0:T(8,128)} %copy.14.tok, f32[1,4096]{1,0:T(1,128)} %bitcast.10, bf16[1544,4096]{1,0:T(8,128)(2,1)} %tab.1), custom_call_target="tpu_custom_call" | custom-call | tf_op jit(solution)/shard_map/head_step/pallas_call | solution.py:674
  537.9 20.1 %hand_over.1 = (f32[1544,4096]{1,0:T(8,128)}, f32[256,4096]{1,0:T(8,128)}, f32[1,4096]{1,0:T(1,128)}, f32[1,1]{1,0:T(1,128)}) custom-call(f32[1544,4096]{1,0:T(8,128)} %get-tuple-element.11.de_in, f32[256,4096]{1,0:T(8,128)} %bitcast.8, f32[1,4352]{1,0:T(1,128)} %get-tuple-element.13.sums_in), custom_call_target="tpu_custom_call" | custom-call | tf_op jit(solution)/shard_map/hand_over/pallas_call | solution.py:692
  (2 shorter events, 0.0 us)
